TPU v7x, 512 devices: a whole 4x8x8 slice. The times are simulated.
512 devices in a mesh: gx: 16 (over z, core), gy: 8 (over y), gz: 4 (over x).
Axes of the slice: x: 4, y: 8, z: 8, core: 2. Of those that a mesh axis runs over, the one named last changes fastest.
Arguments:
- points: float32 [16384, 3, 128], P(('gx', 'gy', 'gz'))
- charges: float32 [16384, 128], P(('gx', 'gy', 'gz')), may hold values from -0.6 to 0.6
- interpolant: float32 [16384, 64, 64], P(('gx', 'gy', 'gz')), may hold values from -0.75 to 0.75
- leaf_transfer: float32 [16384, 64, 64], P(('gx', 'gy', 'gz'))
- node_transfer: float32 [512, 9, 64, 64], P(('gx', 'gy', 'gz')), as said below
- node_points: float32 [512, 9, 3, 64], P(('gx', 'gy', 'gz')), as said below
- near_list: int32 [16384, 8], P(('gx', 'gy', 'gz')), may hold values from 0 to 47, as said below
- near_count: int32 [16384], P(('gx', 'gy', 'gz')), may hold values from 1 to 8, as said below
- far_list: int32 [16384, 8], P(('gx', 'gy', 'gz')), may hold values from 0 to 47, as said below
Outputs:
- potential: float32 [16384, 128], P(('gx', 'gy', 'gz'))
Inputs may be any that keep to these rules, and one draw needn't show every extreme that they name: `near_list`: entry 0 of the list of a leaf with number i within its device is i + 8; the other entries are distinct positions within 8 of i + 8. `far_list`: distinct positions within 8 of the leaf's own position i + 8, none of them in the leaf's near list. Only the first near_count[g] entries of leaf g's near list are used. `node_transfer`: rows of devices in the same node (k, c) are equal at level k. `node_points`: rows of devices in the same node (k, c) are equal at level k.
All inputs are finite; a program needn't handle non-finite values.
Results may differ from a plain program's by a relative error of at most 0.0003.
Values sent between devices are 32-bit elements; how exact they have to be, the bound alone decides.
No kernel may reach another device: no remote copies, remote signals or barrier semaphores. Data moves between devices by JAX's collectives and lax.ppermute only.
A program may use at most 64 MiB of HBM per device.

v0:
```python
import jax
import jax.numpy as jnp
from jax import lax
from jax.sharding import PartitionSpec as P

HALO = 8


SOFTENING = 0.0625
HIGHEST = lax.Precision.HIGHEST


def extended(x, sides, width):
    edges = {}
    for axis, dim in sides:
        count, length = (lax.axis_size(axis), x.shape[dim])
        up = [(i, (i + 1) % count) for i in range(count - 1)]
        last = lax.slice_in_dim(x, length - width, length, axis=dim)
        leading = lax.slice_in_dim(x, 0, width, axis=dim)
        edges[dim] = (
            lax.ppermute(last, axis, up),
            lax.ppermute(leading, axis, [(b, a) for a, b in up]),
        )
    done = []
    for _, dim in sides:
        low, high = edges[dim]
        around = [(width, width) if d in done else (0, 0) for d in range(x.ndim)]
        x = jnp.concatenate([jnp.pad(low, around), x, jnp.pad(high, around)], axis=dim)
        done.append(dim)
    return x


def sent_to_all(x, axis):
    copies = jnp.broadcast_to(x, (lax.axis_size(axis), *x.shape))
    return lax.all_to_all(copies, axis, split_axis=0, concat_axis=0, tiled=True)


def in_order(tiles, dim):
    tiles = jnp.moveaxis(tiles, 0, dim)
    lengths = tiles.shape
    return tiles.reshape(*lengths[:dim], lengths[dim] * lengths[dim + 1], *lengths[dim + 2 :])


def gather_directly(x, axis, dim):
    tiles = sent_to_all(x, axis)
    return in_order(tiles, dim)


def kernel(targets, sources):
    spread = targets[..., :, :, None] - sources[..., :, None, :]
    return lax.rsqrt(jnp.sum(spread * spread, axis=-3) + SOFTENING)


def leaf_terms(window, near_list, near_count, far_list, skeleton_rank):
    leaves = near_list.shape[0]
    margin = (window.shape[0] - leaves) // 2
    targets = window[margin : margin + leaves]
    blocks = leaves // 4

    def block_terms(pieces):
        target_block, near_block, count_block, far_block = pieces
        sources = window[near_block]
        slot_index = jnp.arange(near_block.shape[1], dtype=jnp.int32)
        is_live = slot_index[None, :] < count_block[:, None]
        weights = jnp.where(is_live[:, :, None], sources[:, :, 3, :], 0.0)
        kernel_tiles = kernel(target_block[:, None, 0:3, :], sources[:, :, 0:3, :])
        near_part = jnp.einsum("bmpq,bmq->bp", kernel_tiles, weights, precision=HIGHEST)
        distant = window[far_block]
        coupling = kernel(
            target_block[:, None, 0:3, :skeleton_rank], distant[:, :, 0:3, :skeleton_rank]
        )
        far_part = jnp.einsum(
            "bmpq,bmq->bp", coupling, distant[:, :, 4, :skeleton_rank], precision=HIGHEST
        )
        return (near_part, far_part)

    near_part, far_part = lax.map(
        block_terms,
        (
            targets.reshape((blocks, 4) + targets.shape[1:]),
            near_list.reshape(blocks, 4, near_list.shape[1]),
            near_count.reshape(blocks, 4),
            far_list.reshape(blocks, 4, far_list.shape[1]),
        ),
    )
    return (
        near_part.reshape(leaves, near_part.shape[2]),
        far_part.reshape(leaves, far_part.shape[2]),
    )


def on_device(
    points,
    charges,
    interpolant,
    leaf_transfer,
    node_transfer,
    node_points,
    near_list,
    near_count,
    far_list,
):
    skeleton_rank = interpolant.shape[1]
    leaf_points = points.shape[2]
    skeleton = charges[:, :skeleton_rank] + jnp.einsum(
        "lrp,lp->lr", interpolant, charges[:, skeleton_rank:], precision=HIGHEST
    )
    packed = jnp.concatenate(
        [
            points,
            charges[:, None, :],
            jnp.pad(skeleton, ((0, 0), (0, leaf_points - skeleton_rank)))[:, None, :],
        ],
        axis=1,
    )
    window = extended(packed, ((("gx", "gy", "gz"), 0),), HALO)
    device_skeleton = jnp.einsum("irc,ir->c", leaf_transfer, skeleton, precision=HIGHEST)
    transfers = node_transfer[0]
    centres = node_points[0]
    level_count = transfers.shape[0]
    couplings = []
    gatherers = (
        (
            lax.axis_size("gz"),
            lambda payload: gather_directly(payload, "gz", 0),
            lambda: lax.axis_index("gz"),
        ),
        (
            lax.axis_size("gy"),
            lambda payload: gather_directly(payload, "gy", 0),
            lambda: lax.axis_index("gy"),
        ),
        (
            lax.axis_size("gx"),
            lambda payload: gather_directly(payload, "gx", 0),
            lambda: lax.axis_index("gx"),
        ),
    )
    current = device_skeleton
    level_base = 0
    for axis_length, gatherer, indexer in gatherers:
        bit_count = axis_length.bit_length() - 1
        chain_terms = [current]
        for offset in range(bit_count):
            chain_terms.append(
                jnp.einsum(
                    "rc,r->c", transfers[level_base + offset], chain_terms[-1], precision=HIGHEST
                )
            )
        rows = []
        for offset in range(bit_count):
            rows.append(
                jnp.concatenate([chain_terms[offset][None], centres[level_base + offset]], axis=0)
            )
        rows.append(
            jnp.concatenate(
                [chain_terms[bit_count][None], jnp.zeros((3, skeleton_rank), jnp.float32)], axis=0
            )
        )
        everyone = gatherer(jnp.stack(rows)[None])
        position = indexer()
        for offset in range(bit_count):
            group_size = 2**offset
            group_index = position // group_size
            partner = group_index + 1 - 2 * (group_index % 2)
            members = lax.dynamic_slice_in_dim(
                everyone[:, offset], partner * group_size, group_size, 0
            )
            partner_skeleton = jnp.sum(members[:, 0, :], axis=0)
            couplings.append(
                jnp.dot(
                    kernel(centres[level_base + offset], members[0, 1:4, :]),
                    partner_skeleton,
                    precision=HIGHEST,
                )
            )
        current = jnp.sum(everyone[:, bit_count, 0, :], axis=0)
        level_base = level_base + bit_count
    expansion = couplings[-1]
    for level_index in range(level_count - 1, 0, -1):
        expansion = couplings[level_index - 1] + jnp.dot(
            transfers[level_index - 1], expansion, precision=HIGHEST
        )
    from_device = jnp.einsum("irc,c->ir", leaf_transfer, expansion, precision=HIGHEST)
    near_part, far_part = leaf_terms(window, near_list, near_count, far_list, skeleton_rank)
    combined = far_part + from_device
    upper = jnp.einsum("lrp,lr->lp", interpolant, combined, precision=HIGHEST)
    return jnp.concatenate([combined, upper], axis=1) + near_part


def solution(mesh):
    return jax.shard_map(
        on_device,
        mesh=mesh,
        in_specs=(
            P(("gx", "gy", "gz"), None, None),
            P(("gx", "gy", "gz"), None),
            P(("gx", "gy", "gz"), None, None),
            P(("gx", "gy", "gz"), None, None),
            P(("gx", "gy", "gz"), None, None, None),
            P(("gx", "gy", "gz"), None, None, None),
            P(("gx", "gy", "gz"), None),
            P(("gx", "gy", "gz")),
            P(("gx", "gy", "gz"), None),
        ),
        out_specs=P(("gx", "gy", "gz"), None),
        check_vma=False,
    )
```

profile of v0, /device:TPU:1, one launch (start us, length us, event | category | flops | bytes accessed | tf_op | source)
XLA Modules:
  0.0 111.5 jit_solution(16595539735505145345)
XLA Ops:
  1.7 1.7 %fusion.134 = f32[32,1,64]{2,1,0:T(1,128)S(1)} fusion(f32[32,64,64]{2,1,0:T(8,128)S(1)} %copy-done, f32[32,64,1]{1,2,0:T(1,128)S(1)} %bitcast.414), kind=kOutput, calls=%fused_computation.235 | convolution fusion | flops 1572864 | bytes 540672 | tf_op jit(solution)/shard_map/lrp,lp->lr/dot_general | solution.py:105
  4.1 1.9 %fusion.135 = f32[1,64,1]{1,0,2:T(1,128)S(1)} fusion(f32[32,64,1]{1,2,0:T(1,128)S(1)} %bitcast.408, f32[32,64,64]{2,1,0:T(8,128)} %param.14), kind=kOutput, calls=%fused_computation.236 | convolution fusion | flops 1572864 | bytes 532736 | tf_op jit(solution)/shard_map/irc,ir->c/dot_general | solution.py:117
  7.1 4.8 %all-to-all-start = ((f32[4,1,768]{2,1,0:T(1,128)}), f32[4,1,768]{2,1,0:T(1,128)S(1)}, u32[]{:S(2)}, u32[]{:S(2)}) async-start(f32[4,1,768]{2,1,0:T(1,128)} %reshape.283), calls=%async_computation | async-start | bytes 24576 | tf_op jit(solution)/shard_map/all_to_all | solution.py:35
  12.0 3.4 %collective-permute-start = (f32[8,5,128]{2,1,0:T(8,128)S(1)}, f32[8,5,128]{2,1,0:T(8,128)S(1)}, u32[]{:S(2)}, u32[]{:S(2)}) collective-permute-start(f32[8,5,128]{2,1,0:T(8,128)S(1)} %get-tuple-element.72), channel_id=1, source_target_pairs={{0,1},{1,2},{2,3},{3,4},{4,5},{5,6},{6,7},{7,8},{8,9},{9,10},{10,1... | collective-permute-start | bytes 61448 | tf_op jit(solution)/shard_map/ppermute | solution.py:21
  15.4 7.2 %collective-permute-start.1 = (f32[8,5,128]{2,1,0:T(8,128)S(1)}, f32[8,5,128]{2,1,0:T(8,128)S(1)}, u32[]{:S(2)}, u32[]{:S(2)}) collective-permute-start(f32[8,5,128]{2,1,0:T(8,128)S(1)} %get-tuple-element.73), channel_id=1, source_target_pairs={{1,0},{2,1},{3,2},{4,3},{5,4},{6,5},{7,6},{8,7},{9,8},{10,9},{11,1... | collective-permute-start | bytes 61448 | tf_op jit(solution)/shard_map/ppermute | solution.py:22
  26.2 4.9 %all-to-all-start.1 = ((f32[8,1,1024]{2,1,0:T(1,128)}), f32[8,1,1024]{2,1,0:T(1,128)S(1)}, u32[]{:S(2)}, u32[]{:S(2)}) async-start(f32[8,1,1024]{2,1,0:T(1,128)} %reshape.285), calls=%async_computation.1 | async-start | bytes 65536 | tf_op jit(solution)/shard_map/all_to_all | solution.py:35
  31.3 49.2 %while.12 = (s32[]{:T(128)}, f32[8,4,128]{2,1,0:T(4,128)S(1)}, f32[8,4,64]{2,1,0:T(4,128)S(1)}, f32[8,4,5,128]{3,2,1,0:T(8,128)S(1)}, s32[8,4,8]{2,1,0:T(4,128)S...) while((s32[]{:T(128)}, f32[8,4,128]{2,1,0:T(4,128)S(1)}, ...), condition=%wide.region_3.4_spmd, body=%wide.region_0.3_spmd.sunk | while | flops 13768930 | bytes 6483689 | solution.py:77
  33.5 1.1 fusion.166
  35.4 2.0 %fusion.165 = f32[4,1,128,1]{2,1,3,0:T(1,128)S(1)} fusion(f32[4,8,128,1]{2,3,1,0:T(1,128)S(1)} %bitcast.394, f32[4,8,128,128]{3,2,1,0:T(8,128)S(1)} %multiply_reduce_fusion.13), kind=kOutput, calls=%fused_computation.4.clone.1 | convolution fusion | flops 6815744 | bytes 2115584 | tf_op jit(solution)/shard_map/while/body/eval_jaxpr/bmpq,bmq->bp/dot_general | solution.py:67
  39.6 1.1 fusion.166
  41.5 2.0 %fusion.165 = f32[4,1,128,1]{2,1,3,0:T(1,128)S(1)} fusion(f32[4,8,128,1]{2,3,1,0:T(1,128)S(1)} %bitcast.394, f32[4,8,128,128]{3,2,1,0:T(8,128)S(1)} %multiply_reduce_fusion.13), kind=kOutput, calls=%fused_computation.4.clone.1 | convolution fusion | flops 6815744 | bytes 2115584 | tf_op jit(solution)/shard_map/while/body/eval_jaxpr/bmpq,bmq->bp/dot_general | solution.py:67
  45.8 1.1 fusion.166
  47.7 2.0 %fusion.165 = f32[4,1,128,1]{2,1,3,0:T(1,128)S(1)} fusion(f32[4,8,128,1]{2,3,1,0:T(1,128)S(1)} %bitcast.394, f32[4,8,128,128]{3,2,1,0:T(8,128)S(1)} %multiply_reduce_fusion.13), kind=kOutput, calls=%fused_computation.4.clone.1 | convolution fusion | flops 6815744 | bytes 2115584 | tf_op jit(solution)/shard_map/while/body/eval_jaxpr/bmpq,bmq->bp/dot_general | solution.py:67
  51.9 1.1 fusion.166
  53.8 2.0 %fusion.165 = f32[4,1,128,1]{2,1,3,0:T(1,128)S(1)} fusion(f32[4,8,128,1]{2,3,1,0:T(1,128)S(1)} %bitcast.394, f32[4,8,128,128]{3,2,1,0:T(8,128)S(1)} %multiply_reduce_fusion.13), kind=kOutput, calls=%fused_computation.4.clone.1 | convolution fusion | flops 6815744 | bytes 2115584 | tf_op jit(solution)/shard_map/while/body/eval_jaxpr/bmpq,bmq->bp/dot_general | solution.py:67
  58.1 1.1 fusion.166
  60.0 2.0 %fusion.165 = f32[4,1,128,1]{2,1,3,0:T(1,128)S(1)} fusion(f32[4,8,128,1]{2,3,1,0:T(1,128)S(1)} %bitcast.394, f32[4,8,128,128]{3,2,1,0:T(8,128)S(1)} %multiply_reduce_fusion.13), kind=kOutput, calls=%fused_computation.4.clone.1 | convolution fusion | flops 6815744 | bytes 2115584 | tf_op jit(solution)/shard_map/while/body/eval_jaxpr/bmpq,bmq->bp/dot_general | solution.py:67
  64.2 1.1 fusion.166
  66.1 2.0 %fusion.165 = f32[4,1,128,1]{2,1,3,0:T(1,128)S(1)} fusion(f32[4,8,128,1]{2,3,1,0:T(1,128)S(1)} %bitcast.394, f32[4,8,128,128]{3,2,1,0:T(8,128)S(1)} %multiply_reduce_fusion.13), kind=kOutput, calls=%fused_computation.4.clone.1 | convolution fusion | flops 6815744 | bytes 2115584 | tf_op jit(solution)/shard_map/while/body/eval_jaxpr/bmpq,bmq->bp/dot_general | solution.py:67
  72.3 2.0 %fusion.165 = f32[4,1,128,1]{2,1,3,0:T(1,128)S(1)} fusion(f32[4,8,128,1]{2,3,1,0:T(1,128)S(1)} %bitcast.394, f32[4,8,128,128]{3,2,1,0:T(8,128)S(1)} %multiply_reduce_fusion.13), kind=kOutput, calls=%fused_computation.4.clone.1 | convolution fusion | flops 6815744 | bytes 2115584 | tf_op jit(solution)/shard_map/while/body/eval_jaxpr/bmpq,bmq->bp/dot_general | solution.py:67
  78.5 2.0 %fusion.165 = f32[4,1,128,1]{2,1,3,0:T(1,128)S(1)} fusion(f32[4,8,128,1]{2,3,1,0:T(1,128)S(1)} %bitcast.394, f32[4,8,128,128]{3,2,1,0:T(8,128)S(1)} %multiply_reduce_fusion.13), kind=kOutput, calls=%fused_computation.4.clone.1 | convolution fusion | flops 6815744 | bytes 2115584 | tf_op jit(solution)/shard_map/while/body/eval_jaxpr/bmpq,bmq->bp/dot_general | solution.py:67
  83.4 12.1 %all-to-all-start.2 = ((f32[16,1,1280]{2,1,0:T(1,128)}), f32[16,1,1280]{2,1,0:T(1,128)S(1)}, u32[]{:S(2)}, u32[]{:S(2)}) async-start(f32[16,1,1280]{2,1,0:T(1,128)} %reshape.287), calls=%async_computation.2 | async-start | bytes 163840 | tf_op jit(solution)/shard_map/all_to_all | solution.py:35
  96.0 7.6 %all-to-all-done.2 = f32[16,1,1280]{2,1,0:T(1,128)S(1)} async-done(((f32[16,1,1280]{2,1,0:T(1,128)}), f32[16,1,1280]{2,1,0:T(1,128)S(1)}, u32[]{:S(2)}, u32[]{:S(2)}) %all-to-all-start.2) | async-done | bytes 81952 | tf_op jit(solution)/shard_map/all_to_all | solution.py:35
  107.3 2.5 %fusion.136 = f32[1,32,64]{2,0,1:T(1,128)S(1)} fusion(f32[64,1,1]{0,1,2:T(1,128)S(1)} %fusion.12, f32[32,64,64]{2,1,0:T(8,128)S(1)} %copy-done.1), kind=kOutput, calls=%fused_computation.237 | convolution fusion | flops 1572864 | bytes 532736 | tf_op jit(solution)/shard_map/irc,c->ir/dot_general | solution.py:184
  (293 shorter events, 40.8 us)
Async XLA Ops:
  0.0 1.7 %copy-start = (f32[32,64,64]{2,1,0:T(8,128)S(1)}, f32[32,64,64]{2,1,0:T(8,128)}, u32[]{:S(2)}) copy-start(f32[32,64,64]{2,1,0:T(8,128)} %param.13) | copy-start | bytes 1572868
  0.0 11.9 %copy-start.3 = (f32[32,128]{1,0:T(8,128)S(1)}, f32[32,128]{1,0:T(8,128)}, u32[]{:S(2)}) copy-start(f32[32,128]{1,0:T(8,128)} %param.12) | copy-start | bytes 49156
  0.0 6.0 %copy-start.2 = (f32[1,9,64,64]{3,2,1,0:T(8,128)S(1)}, f32[1,9,64,64]{3,2,1,0:T(8,128)}, u32[]{:S(2)}) copy-start(f32[1,9,64,64]{3,2,1,0:T(8,128)} %param.15) | copy-start | bytes 442372
  0.0 11.9 %copy-start.4 = (f32[32,3,128]{2,0,1:T(8,128)S(1)}, f32[32,3,128]{2,0,1:T(8,128)}, u32[]{:S(2)}) copy-start(f32[32,3,128]{2,0,1:T(8,128)} %param.11) | copy-start | bytes 147460
  0.0 22.9 %copy-start.7 = (s32[32]{0:T(128)S(1)}, s32[32]{0:T(128)}, u32[]{:S(2)}) copy-start(s32[32]{0:T(128)} %param.18) | copy-start | bytes 388
  0.0 23.0 %copy-start.5 = (s32[32,8]{0,1:T(8,128)S(1)}, s32[32,8]{0,1:T(8,128)}, u32[]{:S(2)}) copy-start(s32[32,8]{0,1:T(8,128)} %param.17) | copy-start | bytes 3076
  0.0 23.0 %copy-start.6 = (s32[32,8]{0,1:T(8,128)S(1)}, s32[32,8]{0,1:T(8,128)}, u32[]{:S(2)}) copy-start(s32[32,8]{0,1:T(8,128)} %param.19) | copy-start | bytes 3076
  7.1 16.1 %all-to-all-start = ((f32[4,1,768]{2,1,0:T(1,128)}), f32[4,1,768]{2,1,0:T(1,128)S(1)}, u32[]{:S(2)}, u32[]{:S(2)}) async-start(f32[4,1,768]{2,1,0:T(1,128)} %reshape.283), calls=%async_computation | async-start | bytes 24576 | tf_op jit(solution)/shard_map/all_to_all | solution.py:35
  12.0 19.2 %collective-permute-start = (f32[8,5,128]{2,1,0:T(8,128)S(1)}, f32[8,5,128]{2,1,0:T(8,128)S(1)}, u32[]{:S(2)}, u32[]{:S(2)}) collective-permute-start(f32[8,5,128]{2,1,0:T(8,128)S(1)} %get-tuple-element.72), channel_id=1, source_target_pairs={{0,1},{1,2},{2,3},{3,4},{4,5},{5,6},{6,7},{7,8},{8,9},{9,10},{10,1... | collective-permute-start | bytes 61448 | tf_op jit(solution)/shard_map/ppermute | solution.py:21
  15.4 15.9 %collective-permute-start.1 = (f32[8,5,128]{2,1,0:T(8,128)S(1)}, f32[8,5,128]{2,1,0:T(8,128)S(1)}, u32[]{:S(2)}, u32[]{:S(2)}) collective-permute-start(f32[8,5,128]{2,1,0:T(8,128)S(1)} %get-tuple-element.73), channel_id=1, source_target_pairs={{1,0},{2,1},{3,2},{4,3},{5,4},{6,5},{7,6},{8,7},{9,8},{10,9},{11,1... | collective-permute-start | bytes 61448 | tf_op jit(solution)/shard_map/ppermute | solution.py:22
  26.2 54.4 %all-to-all-start.1 = ((f32[8,1,1024]{2,1,0:T(1,128)}), f32[8,1,1024]{2,1,0:T(1,128)S(1)}, u32[]{:S(2)}, u32[]{:S(2)}) async-start(f32[8,1,1024]{2,1,0:T(1,128)} %reshape.285), calls=%async_computation.1 | async-start | bytes 65536 | tf_op jit(solution)/shard_map/all_to_all | solution.py:35
  80.5 26.8 %copy-start.1 = (f32[32,64,64]{2,1,0:T(8,128)S(1)}, f32[32,64,64]{2,1,0:T(8,128)}, u32[]{:S(2)}) copy-start(f32[32,64,64]{2,1,0:T(8,128)} %param.14) | copy-start | bytes 1572868
  83.4 20.2 %all-to-all-start.2 = ((f32[16,1,1280]{2,1,0:T(1,128)}), f32[16,1,1280]{2,1,0:T(1,128)S(1)}, u32[]{:S(2)}, u32[]{:S(2)}) async-start(f32[16,1,1280]{2,1,0:T(1,128)} %reshape.287), calls=%async_computation.2 | async-start | bytes 163840 | tf_op jit(solution)/shard_map/all_to_all | solution.py:35
where the time goes:
time: 112 us
  matrix products  36.5 us (33%)
  starting transfers between devices  32.4 us (29%)
  other arithmetic  16.8 us (15%)
  local copies, waits for them, and re-layouts  16.6 us (15%)
  waiting for transfers between devices  7.65 us (7%)
    all_to_all x3, starting transfers between devices, sent_to_all(): return lax.all_to_all(copies, axis, split_axis=0, concat_axis=0, tiled=True)  21.8 us
    dot_general x8, matrix products, block_terms(): jnp.einsum('bmpq,bmq->bp', kernel_tiles, weights, precision=HIGHEST)  16.3 us
    reduce_sum x25, other arithmetic, kernel(): return lax.rsqrt(jnp.sum(spread * spread, axis=-3) + SOFTENING)  11.2 us
    dot_general x8, matrix products, block_terms(): jnp.einsum('bmpq,bmq->bp', coupling, distant[:, :, 4, :skeleton_rank], pr...  8.91 us
    all_to_all x3, waiting for transfers between devices, sent_to_all(): return lax.all_to_all(copies, axis, split_axis=0, concat_axis=0, tiled=True)  7.62 us
    ppermute x1, starting transfers between devices, extended(): lax.ppermute(leading, axis, [(b, a) for a, b in up])  7.16 us
    gather x8, local copies, waits for them, and re-layouts, block_terms(): sources = window[near_block]  4.68 us
    gather x8, local copies, waits for them, and re-layouts, block_terms(): distant = window[far_block]  4.68 us
  transfers between devices with their start and end apart: 5, of which 1 were waited for; matrix products, arithmetic and copies ran while one was open for 47% of the time, Pallas kernels for 0%

commit v1 on v0

v1 whole, which is shorter than its diff:
```python
import jax
import jax.numpy as jnp
from jax import lax
from jax.experimental import pallas as pl
from jax.experimental.pallas import tpu as pltpu
from jax.sharding import PartitionSpec as P


HALO = 8
SOFTENING = 0.0625
AXES = ("gx", "gy", "gz")
INTERPRET = False
CHUNKS = 4


class Layout:
    def __init__(self, nx, ny, nz):
        self.nx, self.ny, self.nz = nx, ny, nz
        self.bx, self.by, self.bz = (n.bit_length() - 1 for n in (nx, ny, nz))
        self.levels = self.bx + self.by + self.bz
        self.core = self.bz + self.by
        self.na = 2 * nz
        self.nb = (nx // 2) * ny
        self.low = list(range(self.bz, self.core))
        self.high = list(range(self.core + 1, self.levels))
        both = self.low + self.high
        self.pairs = [both[i : i + 2] for i in range(0, len(both), 2)]
        self.rows_a = 2 + len(self.pairs)
        self.rows_b = 3

    def device(self, a, b):
        gz, core = a % self.nz, a // self.nz
        gy, up = b % self.ny, b // self.ny
        return ((up * 2 + core) * self.ny + gy) * self.nz + gz

    def groups_a(self):
        return [[self.device(a, b) for a in range(self.na)] for b in range(self.nb)]

    def groups_b(self):
        return [[self.device(a, b) for b in range(self.nb)] for a in range(self.na)]

    def level_a(self, diff):
        if diff == 0:
            return 0
        return self.core if diff >= self.nz else diff.bit_length() - 1

    def level_b(self, diff):
        high, low = diff // self.ny, diff % self.ny
        if high:
            return self.core + high.bit_length()
        return self.bz + low.bit_length() - 1 if low else self.bz

    def place(self):
        gx, gy, gz = (lax.axis_index(name) for name in AXES)
        return (gx % 2) * self.nz + gz, (gx // 2) * self.ny + gy


def eye(rows, lanes):
    r = lax.broadcasted_iota(jnp.int32, (rows, lanes), 0)
    c = lax.broadcasted_iota(jnp.int32, (rows, lanes), 1)
    return r == c % rows


def to_row(col, mask):
    return jnp.sum(jnp.where(mask, col, 0.0), axis=0, keepdims=True)


def side(left, right):
    return jnp.concatenate([left, right], axis=1)


def pre_kernel(
    lay, pts_hbm, q_hbm, p_hbm, e_hbm, w_hbm, t_hbm, pack, lo, hi, send, msg, e_ref, p_ref, pts, q, w_ref, t_ref, sem
):
    leaves, rank = w_ref.shape[0], w_ref.shape[1]
    step = leaves // CHUNKS
    small = [
        pltpu.make_async_copy(src, dst, sem.at[2 * CHUNKS + n])
        for n, (src, dst) in enumerate(((q_hbm, q), (pts_hbm, pts), (e_hbm, e_ref), (p_hbm, p_ref)))
    ]
    small[0].start()
    small[1].start()
    copies = []
    for c in range(CHUNKS):
        part = pl.ds(c * step, step)
        copies.append(
            (
                pltpu.make_async_copy(w_hbm.at[part], w_ref.at[part], sem.at[2 * c]),
                pltpu.make_async_copy(t_hbm.at[part], t_ref.at[part], sem.at[2 * c + 1]),
            )
        )
    for w_copy, t_copy in copies:
        w_copy.start()
        t_copy.start()
    small[2].start()
    small[3].start()
    small[0].wait()
    small[1].wait()

    mask = eye(rank, rank)
    mask2 = eye(rank, 2 * rank)
    lane = lax.broadcasted_iota(jnp.int32, (leaves, 2 * rank), 1)
    charge = q[...]
    coords = [pts[c] for c in range(3)]
    twice = [jnp.where(lane < rank, x, pltpu.roll(x, rank, 1)) for x in coords]
    other = pltpu.roll(charge, rank, 1)
    for i in range(leaves):
        for r, x in ((0, coords[0]), (1, coords[1]), (2, coords[2]), (3, charge)):
            pack[i, r : r + 1, :] = x[i : i + 1, :]
        for r in range(3):
            pack[i, 5 + r : 6 + r, :] = twice[r][i : i + 1, :]

    total = jnp.zeros((rank, rank), jnp.float32)
    for c in range(CHUNKS):
        copies[c][0].wait()
        copies[c][1].wait()
        for i in range(c * step, (c + 1) * step):
            own = jnp.where(mask, charge[i : i + 1, :rank], 0.0)
            col = jnp.sum(w_ref[i] * other[i : i + 1, :rank] + own, axis=1, keepdims=True)
            total = total + t_ref[i] * col
            pack[i, 4:5, :] = to_row(col, mask2)
    lo[...] = pack[0:HALO]
    hi[...] = pack[leaves - HALO : leaves]
    small[2].wait()
    small[3].wait()

    rows = [jnp.sum(total, axis=0, keepdims=True)]
    for k in range(0, lay.levels - 1, 2):
        col = jnp.sum(jnp.transpose(e_ref[k]) * rows[k], axis=1, keepdims=True)
        rows.append(to_row(col, mask))
        if k + 2 < lay.levels:
            rows.append(jnp.sum(e_ref[k + 1] * col, axis=0, keepdims=True))

    head = [side(rows[k], p_ref[3 * k]) for k in range(lay.levels)]
    tail = [side(p_ref[3 * k + 1], p_ref[3 * k + 2]) for k in range(lay.levels)]
    sums = [side(rows[pair[0]], rows[pair[-1]]) for pair in lay.pairs]
    for k in range(lay.levels):
        msg[2 * k] = head[k]
        msg[2 * k + 1] = tail[k]
    a, _ = lay.place()
    for diff in range(lay.na):
        base = (a ^ diff) * lay.rows_a
        k = lay.level_a(diff)
        for r, row in enumerate([head[k], tail[k]] + sums):
            send[base + r] = row


def gathered_a(lay, recv, a):
    near, every = [], []
    for j in range(len(lay.pairs)):
        rows = [recv[(a ^ diff) * lay.rows_a + 2 + j] for diff in range(lay.na)]
        part = sum(rows[1 : lay.nz], rows[0])
        near.append(part)
        every.append(sum(rows[lay.nz + 1 :], rows[lay.nz]) + part)
    core = [recv[(a ^ diff) * lay.rows_a] for diff in range(lay.nz, lay.na)]
    return near, every, sum(core[1:], core[0])


def mid_kernel(lay, recv, msg, send):
    rank = msg.shape[2] // 2
    a, b = lay.place()
    near, every, core = gathered_a(lay, recv, a)
    lane = lax.broadcasted_iota(jnp.int32, (1, 2 * rank), 1)
    head = {}
    for j, pair in enumerate(lay.pairs):
        for at, k in enumerate(pair):
            row = near[j] if k < lay.core else every[j]
            if at:
                row = pltpu.roll(row, rank, 1)
            head[k] = jnp.where(lane < rank, row, msg[2 * k])
    tail = {k: msg[2 * k + 1] for k in head}
    for diff in range(lay.nb):
        base = (b ^ diff) * lay.rows_b
        k = lay.level_b(diff)
        send[base] = head[k]
        send[base + 1] = tail[k]
        send[base + 2] = core


def near_kernel(near_list, near_count, far_list, pack, lo, hi, after, near_out, far_out, win, tgt, acc):
    del after
    leaves, lanes = pack.shape[0], pack.shape[2]
    rank = lanes // 2
    tiles = lanes // 8
    far_tiles = rank // 8
    win[0:HALO] = lo[...]
    win[HALO : HALO + leaves] = pack[...]
    win[HALO + leaves :] = hi[...]

    def spread(i, carry):
        cols = jnp.transpose(pack[i])
        for c in range(3):
            tgt[i, c] = jnp.broadcast_to(cols[:, c : c + 1], (lanes, lanes))
        return carry

    lax.fori_loop(0, leaves, spread, 0, unroll=4)

    def kernel_tile(i, t, xs):
        at = pl.ds(8 * t, 8)
        d0 = tgt[i, 0, at, :] - xs[0]
        d1 = tgt[i, 1, at, :] - xs[1]
        d2 = tgt[i, 2, at, :] - xs[2]
        return lax.rsqrt((d0 * d0 + d1 * d1 + d2 * d2) + SOFTENING)

    lane = lax.broadcasted_iota(jnp.int32, (8, lanes), 1)

    def leaf(i, carry):
        def slot(m, sums):
            j = near_list[m, i]
            xs = [jnp.broadcast_to(win[j, pl.ds(c, 1), :], (8, lanes)) for c in range(4)]
            return tuple(sums[t] + kernel_tile(i, t, xs) * xs[3] for t in range(tiles))

        zero = tuple(jnp.zeros((8, lanes), jnp.float32) for _ in range(tiles))
        sums = lax.fori_loop(0, near_count[i], slot, zero)
        for t in range(tiles):
            acc[i, 8 * t : 8 * t + 8, :] = sums[t]

        far = [jnp.zeros((8, lanes), jnp.float32) for _ in range(far_tiles)]
        for m in range(0, far_list.shape[0], 2):
            both = jnp.where(lane < rank, win[far_list[m, i]], win[far_list[m + 1, i]])
            xs = [jnp.broadcast_to(both[r : r + 1, :], (8, lanes)) for r in (5, 6, 7, 4)]
            for t in range(far_tiles):
                far[t] = far[t] + kernel_tile(i, t, xs) * xs[3]
        for t in range(far_tiles):
            fold = far[t] + pltpu.roll(far[t], rank, 1)
            far_out[i, 8 * t : 8 * t + 8, :] = fold[:, :rank]
        return carry

    lax.fori_loop(0, leaves, leaf, 0)

    def reduce(i, carry):
        near_out[i] = jnp.sum(jnp.transpose(acc[i]), axis=0, keepdims=True)
        return carry

    lax.fori_loop(0, leaves, reduce, 0, unroll=4)


def post_kernel(
    lay, recv_a, recv_b, p_ref, e_ref, near, far, w_hbm, t_hbm, out, w_ref, t_ref, p_s, row_s, up_s, sem
):
    leaves, rank = w_ref.shape[0], w_ref.shape[1]
    t_copy = pltpu.make_async_copy(t_hbm, t_ref, sem.at[0])
    w_copy = pltpu.make_async_copy(w_hbm, w_ref, sem.at[1])
    t_copy.start()
    w_copy.start()
    mask = eye(rank, rank)
    a, b = lay.place()
    got_a = lambda diff, r: recv_a[(a ^ diff) * lay.rows_a + r]
    got_b = lambda diff, r: recv_b[(b ^ diff) * lay.rows_b + r]
    for k in range(3 * lay.levels):
        p_s[k : k + 1, :] = p_ref[k]
    own = jnp.transpose(p_s[...])

    weight, first = {}, {}
    for diff in range(1, lay.na):
        k = lay.level_a(diff)
        row = got_a(diff, 0)
        weight[k] = weight[k] + row if k in weight else row
        if k not in first:
            first[k] = (row, got_a(diff, 1))
    for diff in range(1, lay.nb):
        k = lay.level_b(diff)
        row = got_b(diff, 0)
        weight[k] = weight[k] + row if k in weight else row
        if k not in first:
            first[k] = (row, got_b(diff, 1))
        if diff < lay.ny:
            weight[lay.core] = weight[lay.core] + got_b(diff, 2)

    coupling = []
    for k in range(lay.levels):
        top, bottom = first[k]
        xs = [top[:, rank:], bottom[:, :rank], bottom[:, rank:]]
        squares = 0.0
        for c in range(3):
            d = own[:, 3 * k + c : 3 * k + c + 1] - xs[c]
            squares = squares + d * d
        coupling.append(
            jnp.sum(lax.rsqrt(squares + SOFTENING) * weight[k][:, :rank], axis=1, keepdims=True)
        )

    value, is_col = coupling[-1], True
    for k in range(lay.levels - 2, -1, -1):
        if is_col:
            value = jnp.sum(jnp.transpose(e_ref[k]) * value, axis=0, keepdims=True) + to_row(coupling[k], mask)
        else:
            value = jnp.sum(e_ref[k] * value, axis=1, keepdims=True) + coupling[k]
        is_col = not is_col
    row = to_row(value, mask) if is_col else value

    t_copy.wait()
    w_copy.wait()
    for i in range(leaves):
        col = jnp.sum(t_ref[i] * row + far[i], axis=1, keepdims=True)
        row_s[i : i + 1, :] = to_row(col, mask)
        up_s[i : i + 1, :] = jnp.sum(w_ref[i] * col, axis=0, keepdims=True)
    for i in range(leaves):
        out[i : i + 1, :] = near[i]
    out[...] = out[...] + side(row_s[...], up_s[...])


def in_vmem(x):
    return x if INTERPRET else pltpu.with_memory_space_constraint(x, pltpu.VMEM)


def in_hbm(x):
    return x if INTERPRET else pltpu.with_memory_space_constraint(x, pltpu.HBM)


def made(shape):
    return jax.ShapeDtypeStruct(shape, jnp.float32) if INTERPRET else pltpu.VMEM(shape, jnp.float32)


def call(body, in_specs, outs, scratch, flops=0):
    kwargs = {"interpret": True} if INTERPRET else {}
    return pl.pallas_call(
        body,
        in_specs=in_specs,
        out_specs=tuple(pl.BlockSpec(memory_space=pltpu.VMEM) for _ in outs),
        out_shape=tuple(outs),
        scratch_shapes=scratch,
        compiler_params=pltpu.CompilerParams(vmem_limit_bytes=32 << 20),
        cost_estimate=pl.CostEstimate(flops=flops, transcendentals=0, bytes_accessed=1 << 16) if flops else None,
        **kwargs,
    )


VM = pl.BlockSpec(memory_space=pltpu.VMEM)
SM = pl.BlockSpec(memory_space=pltpu.SMEM)
HB = pl.BlockSpec(memory_space=pl.ANY if INTERPRET else pltpu.HBM)


def on_device(
    lay,
    points,
    charges,
    interpolant,
    leaf_transfer,
    node_transfer,
    node_points,
    near_list,
    near_count,
    far_list,
):
    leaves, rank = interpolant.shape[0], interpolant.shape[1]
    lanes = points.shape[2]
    levels = lay.levels
    pts = jnp.transpose(points, (1, 0, 2))
    transfers = node_transfer[0]
    centres = jnp.transpose(node_points, (1, 2, 0, 3)).reshape(3 * levels, 1, rank)
    vec = lambda n: made((n, 1, lanes))
    square = made((leaves, rank, rank))

    pack, lo, hi, send, msg, e_ref, p_ref = call(
        lambda *refs: pre_kernel(lay, *refs),
        [HB] * 6,
        [
            made((leaves, 8, lanes)),
            made((HALO, 8, lanes)),
            made((HALO, 8, lanes)),
            vec(lay.na * lay.rows_a),
            vec(2 * levels),
            made((levels, rank, rank)),
            made((3 * levels, 1, rank)),
        ],
        [
            pltpu.VMEM((3, leaves, lanes), jnp.float32),
            pltpu.VMEM((leaves, lanes), jnp.float32),
            pltpu.VMEM((leaves, rank, rank), jnp.float32),
            pltpu.VMEM((leaves, rank, rank), jnp.float32),
            pltpu.SemaphoreType.DMA((2 * CHUNKS + 4,)),
        ],
    )(*(in_hbm(x) for x in (pts, charges, centres, transfers, interpolant, leaf_transfer)))

    recv_a = lax.all_to_all(send, AXES, 0, 0, axis_index_groups=lay.groups_a(), tiled=True)
    count = lay.na * lay.nb
    up = [(i, i + 1) for i in range(count - 1)]
    low = lax.ppermute(hi, AXES, up)
    high = lax.ppermute(lo, AXES, [(b, a) for a, b in up])

    (send_b,) = call(
        lambda *refs: mid_kernel(lay, *refs), [VM, VM], [vec(lay.nb * lay.rows_b)], []
    )(in_vmem(recv_a), in_vmem(msg))
    recv_b = lax.all_to_all(send_b, AXES, 0, 0, axis_index_groups=lay.groups_b(), tiled=True)

    near, far = call(
        near_kernel,
        [SM, SM, SM, VM, VM, VM, VM],
        [vec(leaves), square],
        [
            pltpu.VMEM((leaves + 2 * HALO, 8, lanes), jnp.float32),
            pltpu.VMEM((leaves, 3, lanes, lanes), jnp.float32),
            pltpu.VMEM((leaves, lanes, lanes), jnp.float32),
        ],
        flops=200_000_000,
    )(near_list.T, near_count, far_list.T, in_vmem(pack), in_vmem(low), in_vmem(high), in_vmem(send_b))

    (out,) = call(
        lambda *refs: post_kernel(lay, *refs),
        [VM] * 6 + [HB] * 2,
        [jax.ShapeDtypeStruct((leaves, lanes), jnp.float32)],
        [
            pltpu.VMEM((leaves, rank, rank), jnp.float32),
            pltpu.VMEM((leaves, rank, rank), jnp.float32),
            pltpu.VMEM((-(-3 * levels // 8) * 8, rank), jnp.float32),
            pltpu.VMEM((leaves, rank), jnp.float32),
            pltpu.VMEM((leaves, rank), jnp.float32),
            pltpu.SemaphoreType.DMA((2,)),
        ],
    )(*(in_vmem(x) for x in (recv_a, recv_b, p_ref, e_ref, near, far)), in_hbm(interpolant), in_hbm(leaf_transfer))
    return out


def solution(mesh):
    lay = Layout(*(mesh.shape[name] for name in AXES))
    split = lambda rest: P(AXES, *([None] * rest))

    def body(*args):
        return on_device(lay, *args)

    return jax.shard_map(
        body,
        mesh=mesh,
        in_specs=(split(2), split(1), split(2), split(2), split(3), split(3), split(1), split(0), split(1)),
        out_specs=split(1),
        check_vma=False,
    )
```

time: 112 us -> 61.9 us (0.55)
  the two profiles are of different devices: /device:TPU:1 before, /device:TPU:63 now
where the time goes in v1:
time: 61.9 us; the launch traced here: 61.5 us
  starting transfers between devices  22.9 us (37%)
  Pallas kernels  22.5 us (36%)
  blocking collectives  7.85 us (13%)
  waiting for transfers between devices  7.52 us (12%)
  local copies, waits for them, and re-layouts  0.66 us (1%)
    all_to_all x1, starting transfers between devices, on_device(): lax.all_to_all(send_b, AXES, 0, 0, axis_index_groups=lay.groups_b(), tile...  15.3 us
    pallas_call x1, Pallas kernels, on_device(): call(near_kernel, [SM, SM, SM, VM, VM, VM, VM], [vec(leaves), square], [p...  15.2 us
    all_to_all x1, blocking collectives, on_device(): lax.all_to_all(send, AXES, 0, 0, axis_index_groups=lay.groups_a(), tiled=...  7.85 us
    ppermute x1, waiting for transfers between devices, on_device(): high = lax.ppermute(lo, AXES, [(b, a) for a, b in up])  7.51 us
    ppermute x1, starting transfers between devices, on_device(): low = lax.ppermute(hi, AXES, up)  5.68 us
    pallas_call x1, Pallas kernels, on_device(): call(lambda *refs: post_kernel(lay, *refs), [VM] * 6 + [HB] * 2, [jax.Sha...  4.1 us
    pallas_call x1, Pallas kernels, on_device(): call(lambda *refs: pre_kernel(lay, *refs), [HB] * 6, [made((leaves, 8, la...  2.37 us
    ppermute x1, starting transfers between devices, on_device(): high = lax.ppermute(lo, AXES, [(b, a) for a, b in up])  1.92 us
  transfers between devices with their start and end apart: 3, of which 1 were waited for; matrix products, arithmetic and copies ran while one was open for 0% of the time, Pallas kernels for 25%

profile of v1, /device:TPU:63, one launch (start us, length us, event | category | flops | bytes accessed | tf_op | source)
XLA Modules:
  0.0 61.5 jit_solution(3909170692852936535)
XLA Ops:
  0.0 2.4 %shard_map.91 = (f32[32,8,128]{2,1,0:T(8,128)S(1)}, f32[8,8,128]{2,1,0:T(8,128)S(1)}, f32[8,8,128]{2,1,0:T(8,128)S(1)}, f32[40,1,128]{2,1,0:T(1,128)S(1)}, f32[1...) custom-call(f32[3,32,128]{2,1,0:T(8,128)} %bitcast.8, f32[32,128]{1,0:T(8,128)} %refs_1_.1, ...), custom_call_target="tpu_custom_call" | custom-call | tf_op jit(solution)/shard_map/pallas_call | solution.py:354
  2.4 7.8 %all_to_all.10.refs_0_ = f32[40,1,128]{2,1,0:T(1,128)S(1)} all-to-all(f32[40,1,128]{2,1,0:T(1,128)S(1)} %get-tuple-element.14), channel_id=1, replica_groups={{0,1,2,3,32,33,34,35},{4,5,6,7,36,37,38,39},{8,9,10,11,40,41,42,43},{12..., dimensions={0} | all-to-all | bytes 40960 | tf_op jit(solution)/shard_map/all_to_all | solution.py:375
  10.2 0.8 %shard_map.92.after = f32[192,1,128]{2,1,0:T(1,128)} custom-call(f32[40,1,128]{2,1,0:T(1,128)S(1)} %all_to_all.10.refs_0_, f32[18,1,128]{2,1,0:T(1,128)S(1)} %get-tuple-element.15.refs_1_), custom_call_target="tpu_custom_call" | custom-call | tf_op jit(solution)/shard_map/pallas_call | solution.py:381
  11.0 15.3 %all-to-all-start.1 = ((f32[192,1,128]{2,1,0:T(1,128)}), f32[192,1,128]{2,1,0:T(1,128)S(1)}, u32[]{:S(2)}, u32[]{:S(2)}) async-start(f32[192,1,128]{2,1,0:T(1,128)} %shard_map.92.after), calls=%async_computation.1 | async-start | bytes 196608 | tf_op jit(solution)/shard_map/all_to_all | solution.py:384
  26.3 0.0 copy-start.1
  26.4 0.0 copy-start
  26.4 5.7 %collective-permute-start = (f32[8,8,128]{2,1,0:T(8,128)S(1)}, f32[8,8,128]{2,1,0:T(8,128)S(1)}, u32[]{:S(2)}, u32[]{:S(2)}) collective-permute-start(f32[8,8,128]{2,1,0:T(8,128)S(1)} %get-tuple-element.19), channel_id=1, source_target_pairs={{0,1},{1,2},{2,3},{3,4},{4,5},{5,6},{6,7},{7,8},{8,9},{9,10},{10,1... | collective-permute-start | bytes 98312 | tf_op jit(solution)/shard_map/ppermute | solution.py:378
  32.1 1.9 %collective-permute-start.1 = (f32[8,8,128]{2,1,0:T(8,128)S(1)}, f32[8,8,128]{2,1,0:T(8,128)S(1)}, u32[]{:S(2)}, u32[]{:S(2)}) collective-permute-start(f32[8,8,128]{2,1,0:T(8,128)S(1)} %get-tuple-element.20), channel_id=1, source_target_pairs={{1,0},{2,1},{3,2},{4,3},{5,4},{6,5},{7,6},{8,7},{9,8},{10,9},{11,1... | collective-permute-start | bytes 98312 | tf_op jit(solution)/shard_map/ppermute | solution.py:379
  34.0 0.0 collective-permute-done.lo
  34.0 7.5 %collective-permute-done.1.hi = f32[8,8,128]{2,1,0:T(8,128)S(1)} collective-permute-done((f32[8,8,128]{2,1,0:T(8,128)S(1)}, f32[8,8,128]{2,1,0:T(8,128)S(1)}, u32[]{:S(2)}, u32[]{:S(2)}) %collective-permute-start.1) | collective-permute-done | bytes 32800 | tf_op jit(solution)/shard_map/ppermute | solution.py:379
  41.5 0.0 copy-start.2
  41.5 0.0 copy-done.1
  41.5 0.0 copy-done
  41.5 0.6 %copy-done.2 = s32[32]{0:T(128)S(1)} copy-done((s32[32]{0:T(128)S(1)}, s32[32]{0:T(128)}, u32[]{:S(2)}) %copy-start.2) | copy-done | bytes 152
  42.2 15.2 %shard_map.93 = (f32[32,1,128]{2,1,0:T(1,128)S(1)}, f32[32,64,64]{2,1,0:T(8,128)S(1)}) custom-call(s32[8,32]{1,0:T(8,128)S(1)} %bitcast.5, s32[32]{0:T(128)S(1)} %copy-done.2, s32[8,32]{1,0:T(8,128)S(1)} %bitcast.6, f32[32,8,128]{2,1,0:T(8,128)S(1)} %get-tuple-element.18.pack, f32[8,8,128]{2,1,0:T(8,128)S(1)} %collective-permute-done.lo, ...), custom_call_target="tpu_custom_call" | custom-call | flops 200000000 | bytes 65536 | tf_op jit(solution)/shard_map/pallas_call | solution.py:386
  57.4 0.0 all-to-all-done.1.refs_1_
  57.4 4.1 %shard_map.94 = f32[32,128]{1,0:T(8,128)} custom-call(f32[40,1,128]{2,1,0:T(1,128)S(1)} %all_to_all.10.refs_0_, f32[192,1,128]{2,1,0:T(1,128)S(1)} %all-to-all-done.1.refs_1_, f32[27,1,64]{2,1,0:T(1,128)S(1)} %get-tuple-element.16.refs_2_, f32[9,64,64]{2,1,0:T(8,128)S(1)} %get-tuple-element.17.refs_3_, f32[32,1,128]{2,1,0:T(1,128)S(1)} %get-tuple-element.21.refs_4_, ...), custom_call_target="tpu_custom_call" | custom-call | tf_op jit(solution)/shard_map/pallas_call | solution.py:398
Async XLA Ops:
  11.0 46.4 %all-to-all-start.1 = ((f32[192,1,128]{2,1,0:T(1,128)}), f32[192,1,128]{2,1,0:T(1,128)S(1)}, u32[]{:S(2)}, u32[]{:S(2)}) async-start(f32[192,1,128]{2,1,0:T(1,128)} %shard_map.92.after), calls=%async_computation.1 | async-start | bytes 196608 | tf_op jit(solution)/shard_map/all_to_all | solution.py:384
  26.3 15.2 %copy-start.1 = (s32[32,8]{0,1:T(8,128)S(1)}, s32[32,8]{0,1:T(8,128)}, u32[]{:S(2)}) copy-start(s32[32,8]{0,1:T(8,128)} %param.17) | copy-start | bytes 3076
  26.4 15.2 %copy-start = (s32[32,8]{0,1:T(8,128)S(1)}, s32[32,8]{0,1:T(8,128)}, u32[]{:S(2)}) copy-start(s32[32,8]{0,1:T(8,128)} %param.15) | copy-start | bytes 3076
  26.4 7.6 %collective-permute-start = (f32[8,8,128]{2,1,0:T(8,128)S(1)}, f32[8,8,128]{2,1,0:T(8,128)S(1)}, u32[]{:S(2)}, u32[]{:S(2)}) collective-permute-start(f32[8,8,128]{2,1,0:T(8,128)S(1)} %get-tuple-element.19), channel_id=1, source_target_pairs={{0,1},{1,2},{2,3},{3,4},{4,5},{5,6},{6,7},{7,8},{8,9},{9,10},{10,1... | collective-permute-start | bytes 98312 | tf_op jit(solution)/shard_map/ppermute | solution.py:378
  32.1 9.5 %collective-permute-start.1 = (f32[8,8,128]{2,1,0:T(8,128)S(1)}, f32[8,8,128]{2,1,0:T(8,128)S(1)}, u32[]{:S(2)}, u32[]{:S(2)}) collective-permute-start(f32[8,8,128]{2,1,0:T(8,128)S(1)} %get-tuple-element.20), channel_id=1, source_target_pairs={{1,0},{2,1},{3,2},{4,3},{5,4},{6,5},{7,6},{8,7},{9,8},{10,9},{11,1... | collective-permute-start | bytes 98312 | tf_op jit(solution)/shard_map/ppermute | solution.py:379
  41.5 0.7 %copy-start.2 = (s32[32]{0:T(128)S(1)}, s32[32]{0:T(128)}, u32[]{:S(2)}) copy-start(s32[32]{0:T(128)} %near_count.1) | copy-start | bytes 388

commit v2 on v1

--- a/solution.py
+++ b/solution.py
@@ -11,6 +11,8 @@
 AXES = ("gx", "gy", "gz")
 INTERPRET = False
 CHUNKS = 4
+UNROLL = 4
+FINISH = 4
 
 
 class Layout:
@@ -70,13 +72,23 @@
 
 
 def pre_kernel(
-    lay, pts_hbm, q_hbm, p_hbm, e_hbm, w_hbm, t_hbm, pack, lo, hi, send, msg, e_ref, p_ref, pts, q, w_ref, t_ref, sem
+    lay, pts_hbm, q_hbm, p_hbm, e_hbm, w_hbm, t_hbm, l1_hbm, l2_hbm, l3_hbm,
+    pack, lo, hi, send, msg, e_ref, p_ref, l1, l2, l3, pts, q, w_ref, t_ref, sem,
 ):
     leaves, rank = w_ref.shape[0], w_ref.shape[1]
     step = leaves // CHUNKS
     small = [
         pltpu.make_async_copy(src, dst, sem.at[2 * CHUNKS + n])
-        for n, (src, dst) in enumerate(((q_hbm, q), (pts_hbm, pts), (e_hbm, e_ref), (p_hbm, p_ref)))
+        for n, (src, dst) in enumerate((
+            (q_hbm, q),
+            (pts_hbm, pts),
+            (e_hbm, e_ref),
+            (p_hbm, p_ref),
+            (l1_hbm, l1),
+            (l2_hbm, l2),
+            (l3_hbm, l3),
+        )
+        )
     ]
     small[0].start()
     small[1].start()
@@ -92,8 +104,8 @@
     for w_copy, t_copy in copies:
         w_copy.start()
         t_copy.start()
-    small[2].start()
-    small[3].start()
+    for copy in small[2:]:
+        copy.start()
     small[0].wait()
     small[1].wait()
 
@@ -121,8 +133,8 @@
             pack[i, 4:5, :] = to_row(col, mask2)
     lo[...] = pack[0:HALO]
     hi[...] = pack[leaves - HALO : leaves]
-    small[2].wait()
-    small[3].wait()
+    for copy in small[2:]:
+        copy.wait()
 
     rows = [jnp.sum(total, axis=0, keepdims=True)]
     for k in range(0, lay.levels - 1, 2):
@@ -156,7 +168,7 @@
     return near, every, sum(core[1:], core[0])
 
 
-def mid_kernel(lay, recv, msg, send):
+def mid_kernel(lay, recv, msg, send, token):
     rank = msg.shape[2] // 2
     a, b = lay.place()
     near, every, core = gathered_a(lay, recv, a)
@@ -175,10 +187,28 @@
         send[base] = head[k]
         send[base + 1] = tail[k]
         send[base + 2] = core
-
-
-def near_kernel(near_list, near_count, far_list, pack, lo, hi, after, near_out, far_out, win, tgt, acc):
+    token[0] = core
+
+
+def near_kernel(
+    near_src, count_src, far_src, pack, lo, hi, after, t_hbm, w_hbm,
+    near_out, far_out, w_out, near_list, near_count, far_list, win, tgt, acc, t_ref, sem,
+):
     del after
+    copies = [
+        pltpu.make_async_copy(src, dst, sem.at[n])
+        for n, (src, dst) in enumerate(
+            (
+                (near_src, near_list),
+                (count_src, near_count),
+                (far_src, far_list),
+                (t_hbm, t_ref),
+                (w_hbm, w_out),
+            )
+        )
+    ]
+    for copy in copies:
+        copy.start()
     leaves, lanes = pack.shape[0], pack.shape[2]
     rank = lanes // 2
     tiles = lanes // 8
@@ -187,62 +217,100 @@
     win[HALO : HALO + leaves] = pack[...]
     win[HALO + leaves :] = hi[...]
 
-    def spread(i, carry):
-        cols = jnp.transpose(pack[i])
+    pick = lax.broadcasted_iota(jnp.int32, (32, 3 * lanes), 0) % 8
+    wide = lax.broadcasted_iota(jnp.int32, (32, 3 * lanes), 1) // lanes
+    choose = jnp.where(pick == wide, 1.0, 0.0).astype(jnp.bfloat16)
+    used = lax.broadcasted_iota(jnp.int32, (8, lanes), 0) < 3
+
+    def spread(i):
+        x = jnp.where(used, win[HALO + i], 0.0)
+        high = x.astype(jnp.bfloat16).astype(jnp.float32)
+        rest = x - high
+        mid = rest.astype(jnp.bfloat16).astype(jnp.float32)
+        parts = jnp.concatenate([high, mid, rest - mid, jnp.zeros_like(x)], axis=0)
+        cols = jnp.transpose(parts).astype(jnp.bfloat16)
+        out = jnp.dot(cols, choose, preferred_element_type=jnp.float32)
+        return [out[:, c * lanes : (c + 1) * lanes] for c in range(3)]
+
+    def keep(i, cols):
         for c in range(3):
-            tgt[i, c] = jnp.broadcast_to(cols[:, c : c + 1], (lanes, lanes))
-        return carry
-
-    lax.fori_loop(0, leaves, spread, 0, unroll=4)
-
-    def kernel_tile(i, t, xs):
+            tgt[i, c] = cols[c]
+
+    for i in range(UNROLL):
+        keep(i, spread(i))
+    for copy in copies[:3]:
+        copy.wait()
+
+    def weighted(i, t, xs):
         at = pl.ds(8 * t, 8)
         d0 = tgt[i, 0, at, :] - xs[0]
         d1 = tgt[i, 1, at, :] - xs[1]
         d2 = tgt[i, 2, at, :] - xs[2]
-        return lax.rsqrt((d0 * d0 + d1 * d1 + d2 * d2) + SOFTENING)
+        return lax.rsqrt((d0 * d0 + d1 * d1 + d2 * d2) + SOFTENING) * xs[3]
+
+    def rows(j, which):
+        return [jnp.broadcast_to(win[j, pl.ds(r, 1), :], (8, lanes)) for r in which]
 
     lane = lax.broadcasted_iota(jnp.int32, (8, lanes), 1)
 
+    def far_field(g, carry):
+        ahead = [spread((g + 1) * UNROLL + u) for u in range(UNROLL)]
+        for u in range(UNROLL):
+            i = g * UNROLL + u
+            both = []
+            for m in range(0, far_list.shape[0], 2):
+                block = jnp.where(lane < rank, win[far_list[m, i]], win[far_list[m + 1, i]])
+                both.append([jnp.broadcast_to(block[r : r + 1, :], (8, lanes)) for r in (5, 6, 7, 4)])
+            for t in range(far_tiles):
+                far = weighted(i, t, both[0])
+                for xs in both[1:]:
+                    far = far + weighted(i, t, xs)
+                far_out[i, pl.ds(8 * t, 8), :] = far + pltpu.roll(far, rank, 1)
+        for u in range(UNROLL):
+            i = (g + 1) * UNROLL + u
+            keep(i, ahead[u])
+        return carry
+
+    lax.fori_loop(0, leaves // UNROLL, far_field, 0)
+
     def leaf(i, carry):
-        def slot(m, sums):
-            j = near_list[m, i]
-            xs = [jnp.broadcast_to(win[j, pl.ds(c, 1), :], (8, lanes)) for c in range(4)]
-            return tuple(sums[t] + kernel_tile(i, t, xs) * xs[3] for t in range(tiles))
-
-        zero = tuple(jnp.zeros((8, lanes), jnp.float32) for _ in range(tiles))
-        sums = lax.fori_loop(0, near_count[i], slot, zero)
+        count = near_count[i]
         for t in range(tiles):
-            acc[i, 8 * t : 8 * t + 8, :] = sums[t]
-
-        far = [jnp.zeros((8, lanes), jnp.float32) for _ in range(far_tiles)]
-        for m in range(0, far_list.shape[0], 2):
-            both = jnp.where(lane < rank, win[far_list[m, i]], win[far_list[m + 1, i]])
-            xs = [jnp.broadcast_to(both[r : r + 1, :], (8, lanes)) for r in (5, 6, 7, 4)]
-            for t in range(far_tiles):
-                far[t] = far[t] + kernel_tile(i, t, xs) * xs[3]
+            acc[i, pl.ds(8 * t, 8), :] = jnp.zeros((8, lanes), jnp.float32)
+
+        def slots(n, inner):
+            m = 2 * n + 1
+            one = rows(near_list[m, i], range(4))
+            then = jnp.minimum(m + 1, near_list.shape[0] - 1)
+            two = rows(near_list[then, i], range(4))
+            two[3] = two[3] * jnp.where(m + 1 < count, 1.0, 0.0)
+            for t in range(tiles):
+                at = pl.ds(8 * t, 8)
+                acc[i, at, :] = acc[i, at, :] + (weighted(i, t, one) + weighted(i, t, two))
+            return inner
+
+        return lax.fori_loop(0, count // 2, slots, carry)
+
+    lax.fori_loop(0, leaves, leaf, 0)
+    copies[3].wait()
+
+    def finish(i, carry):
+        own = rows(near_list[0, i], range(4))
+        sums = [acc[i, pl.ds(8 * t, 8), :] + weighted(i, t, own) for t in range(tiles)]
+        whole = jnp.concatenate(sums, axis=0)
+        near_out[i] = jnp.sum(jnp.transpose(whole), axis=0, keepdims=True)
         for t in range(far_tiles):
-            fold = far[t] + pltpu.roll(far[t], rank, 1)
-            far_out[i, 8 * t : 8 * t + 8, :] = fold[:, :rank]
+            at = pl.ds(8 * t, 8)
+            tile = t_ref[i, at, :]
+            far_out[i, at, :] = jnp.where(lane < rank, side(tile, tile), far_out[i, at, :])
         return carry
 
-    lax.fori_loop(0, leaves, leaf, 0)
-
-    def reduce(i, carry):
-        near_out[i] = jnp.sum(jnp.transpose(acc[i]), axis=0, keepdims=True)
-        return carry
-
-    lax.fori_loop(0, leaves, reduce, 0, unroll=4)
-
-
-def post_kernel(
-    lay, recv_a, recv_b, p_ref, e_ref, near, far, w_hbm, t_hbm, out, w_ref, t_ref, p_s, row_s, up_s, sem
-):
+    lax.fori_loop(0, leaves, finish, 0, unroll=FINISH)
+    copies[4].wait()
+
+
+def post_kernel(lay, recv_a, recv_b, p_ref, e_ref, near, far, w_ref, out, p_s, row_s, up_s):
     leaves, rank = w_ref.shape[0], w_ref.shape[1]
-    t_copy = pltpu.make_async_copy(t_hbm, t_ref, sem.at[0])
-    w_copy = pltpu.make_async_copy(w_hbm, w_ref, sem.at[1])
-    t_copy.start()
-    w_copy.start()
     mask = eye(rank, rank)
     a, b = lay.place()
     got_a = lambda diff, r: recv_a[(a ^ diff) * lay.rows_a + r]
@@ -286,12 +354,12 @@
         else:
             value = jnp.sum(e_ref[k] * value, axis=1, keepdims=True) + coupling[k]
         is_col = not is_col
-    row = to_row(value, mask) if is_col else value
-
-    t_copy.wait()
-    w_copy.wait()
+    row = to_row(value, eye(rank, 2 * rank)) if is_col else side(value, value)
+    lane = lax.broadcasted_iota(jnp.int32, (1, 2 * rank), 1)
+    row = jnp.where(lane < rank, row, 1.0)
+
     for i in range(leaves):
-        col = jnp.sum(t_ref[i] * row + far[i], axis=1, keepdims=True)
+        col = jnp.sum(far[i] * row, axis=1, keepdims=True)
         row_s[i : i + 1, :] = to_row(col, mask)
         up_s[i : i + 1, :] = jnp.sum(w_ref[i] * col, axis=0, keepdims=True)
     for i in range(leaves):
@@ -307,8 +375,8 @@
     return x if INTERPRET else pltpu.with_memory_space_constraint(x, pltpu.HBM)
 
 
-def made(shape):
-    return jax.ShapeDtypeStruct(shape, jnp.float32) if INTERPRET else pltpu.VMEM(shape, jnp.float32)
+def made(shape, dtype=jnp.float32):
+    return jax.ShapeDtypeStruct(shape, dtype) if INTERPRET else pltpu.VMEM(shape, dtype)
 
 
 def call(body, in_specs, outs, scratch, flops=0):
@@ -348,12 +416,12 @@
     pts = jnp.transpose(points, (1, 0, 2))
     transfers = node_transfer[0]
     centres = jnp.transpose(node_points, (1, 2, 0, 3)).reshape(3 * levels, 1, rank)
+    tables = (near_list.T, near_count, far_list.T)
     vec = lambda n: made((n, 1, lanes))
-    square = made((leaves, rank, rank))
-
-    pack, lo, hi, send, msg, e_ref, p_ref = call(
+
+    pack, lo, hi, send, msg, e_ref, p_ref, *lists = call(
         lambda *refs: pre_kernel(lay, *refs),
-        [HB] * 6,
+        [HB] * 9,
         [
             made((leaves, 8, lanes)),
             made((HALO, 8, lanes)),
@@ -362,15 +430,16 @@
             vec(2 * levels),
             made((levels, rank, rank)),
             made((3 * levels, 1, rank)),
+            *(made(x.shape, jnp.int32) for x in tables),
         ],
         [
             pltpu.VMEM((3, leaves, lanes), jnp.float32),
             pltpu.VMEM((leaves, lanes), jnp.float32),
             pltpu.VMEM((leaves, rank, rank), jnp.float32),
             pltpu.VMEM((leaves, rank, rank), jnp.float32),
-            pltpu.SemaphoreType.DMA((2 * CHUNKS + 4,)),
+            pltpu.SemaphoreType.DMA((2 * CHUNKS + 7,)),
         ],
-    )(*(in_hbm(x) for x in (pts, charges, centres, transfers, interpolant, leaf_transfer)))
+    )(*(in_hbm(x) for x in (pts, charges, centres, transfers, interpolant, leaf_transfer, *tables)))
 
     recv_a = lax.all_to_all(send, AXES, 0, 0, axis_index_groups=lay.groups_a(), tiled=True)
     count = lay.na * lay.nb
@@ -378,37 +447,50 @@
     low = lax.ppermute(hi, AXES, up)
     high = lax.ppermute(lo, AXES, [(b, a) for a, b in up])
 
-    (send_b,) = call(
-        lambda *refs: mid_kernel(lay, *refs), [VM, VM], [vec(lay.nb * lay.rows_b)], []
+    send_b, token = call(
+        lambda *refs: mid_kernel(lay, *refs), [VM, VM], [vec(lay.nb * lay.rows_b), vec(1)], []
     )(in_vmem(recv_a), in_vmem(msg))
     recv_b = lax.all_to_all(send_b, AXES, 0, 0, axis_index_groups=lay.groups_b(), tiled=True)
 
-    near, far = call(
-        near_kernel,
-        [SM, SM, SM, VM, VM, VM, VM],
-        [vec(leaves), square],
-        [
-            pltpu.VMEM((leaves + 2 * HALO, 8, lanes), jnp.float32),
-            pltpu.VMEM((leaves, 3, lanes, lanes), jnp.float32),
-            pltpu.VMEM((leaves, lanes, lanes), jnp.float32),
-        ],
-        flops=200_000_000,
-    )(near_list.T, near_count, far_list.T, in_vmem(pack), in_vmem(low), in_vmem(high), in_vmem(send_b))
+    near, far, w_ref = near_call(
+        *lists, pack, low, high, token, leaf_transfer, interpolant
+    )
 
     (out,) = call(
         lambda *refs: post_kernel(lay, *refs),
-        [VM] * 6 + [HB] * 2,
+        [VM] * 7,
         [jax.ShapeDtypeStruct((leaves, lanes), jnp.float32)],
         [
-            pltpu.VMEM((leaves, rank, rank), jnp.float32),
-            pltpu.VMEM((leaves, rank, rank), jnp.float32),
             pltpu.VMEM((-(-3 * levels // 8) * 8, rank), jnp.float32),
             pltpu.VMEM((leaves, rank), jnp.float32),
             pltpu.VMEM((leaves, rank), jnp.float32),
-            pltpu.SemaphoreType.DMA((2,)),
         ],
-    )(*(in_vmem(x) for x in (recv_a, recv_b, p_ref, e_ref, near, far)), in_hbm(interpolant), in_hbm(leaf_transfer))
+    )(*(in_vmem(x) for x in (recv_a, recv_b, p_ref, e_ref, near, far, w_ref)))
     return out
+
+
+def near_call(near_list, near_count, far_list, pack, low, high, token, leaf_transfer, interpolant):
+    leaves, rank = interpolant.shape[0], interpolant.shape[1]
+    lanes = pack.shape[2]
+    return call(
+        near_kernel,
+        [VM] * 7 + [HB] * 2,
+        [made((leaves, 1, lanes)), made((leaves, rank, lanes)), made((leaves, rank, rank))],
+        [
+            pltpu.SMEM(near_list.shape, jnp.int32),
+            pltpu.SMEM(near_count.shape, jnp.int32),
+            pltpu.SMEM(far_list.shape, jnp.int32),
+            pltpu.VMEM((leaves + 2 * HALO, 8, lanes), jnp.float32),
+            pltpu.VMEM((leaves + UNROLL, 3, lanes, lanes), jnp.float32),
+            pltpu.VMEM((leaves, lanes, lanes), jnp.float32),
+            pltpu.VMEM((leaves, rank, rank), jnp.float32),
+            pltpu.SemaphoreType.DMA((5,)),
+        ],
+        flops=200_000_000,
+    )(
+        *(in_vmem(x) for x in (near_list, near_count, far_list, pack, low, high, token)),
+        *(in_hbm(x) for x in (leaf_transfer, interpolant)),
+    )
 
 
 def solution(mesh):

time: 61.9 us -> 55.6 us (0.90)
  Pallas kernels: 22.5 us -> 16.9 us
  local copies, waits for them, and re-layouts: 0.66 us -> 0 us
    pallas_call x3, Pallas kernels: 21.7 us -> 16.1 us  [the longest x1 10.1 us: near_call(): call(near_kernel, [VM] * 7 + [HB] * 2, [made((leaves, 1, lanes)), made((l...]
    unnamed x6 -> x0, local copies, waits for them, and re-layouts: 0.66 us -> none
  transfers between devices with their start and end apart: 3 -> 3, of which waited for: 1 -> 1; matrix products, arithmetic and copies ran while one was open for 0% -> 0% of each run, Pallas kernels for 25% -> 18%
where the time goes in v2:
time: 55.6 us; the launch traced here: 55.3 us
  starting transfers between devices  22.9 us (41%)
  Pallas kernels  16.9 us (30%)
  blocking collectives  7.85 us (14%)
  waiting for transfers between devices  7.52 us (14%)
    all_to_all x1, starting transfers between devices, on_device(): lax.all_to_all(send_b, AXES, 0, 0, axis_index_groups=lay.groups_b(), tile...  15.3 us
    pallas_call x1, Pallas kernels, near_call(): call(near_kernel, [VM] * 7 + [HB] * 2, [made((leaves, 1, lanes)), made((l...  10.1 us
    all_to_all x1, blocking collectives, on_device(): lax.all_to_all(send, AXES, 0, 0, axis_index_groups=lay.groups_a(), tiled=...  7.85 us
    ppermute x1, waiting for transfers between devices, on_device(): high = lax.ppermute(lo, AXES, [(b, a) for a, b in up])  7.51 us
    ppermute x1, starting transfers between devices, on_device(): low = lax.ppermute(hi, AXES, up)  5.68 us
    pallas_call x1, Pallas kernels, on_device(): call(lambda *refs: post_kernel(lay, *refs), [VM] * 7, [jax.ShapeDtypeStru...  3.61 us
    pallas_call x1, Pallas kernels, on_device(): call(lambda *refs: pre_kernel(lay, *refs), [HB] * 9, [made((leaves, 8, la...  2.4 us
    ppermute x1, starting transfers between devices, on_device(): high = lax.ppermute(lo, AXES, [(b, a) for a, b in up])  1.92 us
  transfers between devices with their start and end apart: 3, of which 1 were waited for; matrix products, arithmetic and copies ran while one was open for 0% of the time, Pallas kernels for 18%

profile of v2, /device:TPU:63, one launch (start us, length us, event | category | flops | bytes accessed | tf_op | source)
XLA Modules:
  0.0 55.3 jit_solution(18079649693420139690)
XLA Ops:
  0.0 2.4 %shard_map.91 = (f32[32,8,128]{2,1,0:T(8,128)S(1)}, f32[8,8,128]{2,1,0:T(8,128)S(1)}, f32[8,8,128]{2,1,0:T(8,128)S(1)}, f32[40,1,128]{2,1,0:T(1,128)S(1)}, f32[1...) custom-call(f32[3,32,128]{2,1,0:T(8,128)} %bitcast.6, ...), custom_call_target="tpu_custom_call" | custom-call | tf_op jit(solution)/shard_map/pallas_call | solution.py:422
  2.4 7.8 %all_to_all.10.refs_0_ = f32[40,1,128]{2,1,0:T(1,128)S(1)} all-to-all(f32[40,1,128]{2,1,0:T(1,128)S(1)} %get-tuple-element.20), channel_id=1, replica_groups={{0,1,2,3,32,33,34,35},{4,5,6,7,36,37,38,39},{8,9,10,11,40,41,42,43},{12..., dimensions={0} | all-to-all | bytes 40960 | tf_op jit(solution)/shard_map/all_to_all | solution.py:444
  10.2 0.8 %shard_map.92 = (f32[192,1,128]{2,1,0:T(1,128)}, f32[1,1,128]{2,1,0:T(1,128)S(1)}) custom-call(f32[40,1,128]{2,1,0:T(1,128)S(1)} %all_to_all.10.refs_0_, f32[18,1,128]{2,1,0:T(1,128)S(1)} %get-tuple-element.21.refs_1_), custom_call_target="tpu_custom_call" | custom-call | tf_op jit(solution)/shard_map/pallas_call | solution.py:450
  11.0 15.3 %all-to-all-start.1 = ((f32[192,1,128]{2,1,0:T(1,128)}), f32[192,1,128]{2,1,0:T(1,128)S(1)}, u32[]{:S(2)}, u32[]{:S(2)}) async-start(f32[192,1,128]{2,1,0:T(1,128)} %get-tuple-element.22), calls=%async_computation.1 | async-start | bytes 196608 | tf_op jit(solution)/shard_map/all_to_all | solution.py:453
  26.4 5.7 %collective-permute-start = (f32[8,8,128]{2,1,0:T(8,128)S(1)}, f32[8,8,128]{2,1,0:T(8,128)S(1)}, u32[]{:S(2)}, u32[]{:S(2)}) collective-permute-start(f32[8,8,128]{2,1,0:T(8,128)S(1)} %get-tuple-element.29), channel_id=1, source_target_pairs={{0,1},{1,2},{2,3},{3,4},{4,5},{5,6},{6,7},{7,8},{8,9},{9,10},{10,1... | collective-permute-start | bytes 98312 | tf_op jit(solution)/shard_map/ppermute | solution.py:447
  32.1 1.9 %collective-permute-start.1 = (f32[8,8,128]{2,1,0:T(8,128)S(1)}, f32[8,8,128]{2,1,0:T(8,128)S(1)}, u32[]{:S(2)}, u32[]{:S(2)}) collective-permute-start(f32[8,8,128]{2,1,0:T(8,128)S(1)} %get-tuple-element.30), channel_id=1, source_target_pairs={{1,0},{2,1},{3,2},{4,3},{5,4},{6,5},{7,6},{8,7},{9,8},{10,9},{11,1... | collective-permute-start | bytes 98312 | tf_op jit(solution)/shard_map/ppermute | solution.py:448
  34.0 0.0 collective-permute-done.lo
  34.0 7.5 %collective-permute-done.1.hi = f32[8,8,128]{2,1,0:T(8,128)S(1)} collective-permute-done((f32[8,8,128]{2,1,0:T(8,128)S(1)}, f32[8,8,128]{2,1,0:T(8,128)S(1)}, u32[]{:S(2)}, u32[]{:S(2)}) %collective-permute-start.1) | collective-permute-done | bytes 32800 | tf_op jit(solution)/shard_map/ppermute | solution.py:448
  41.5 10.1 %shard_map.93 = (f32[32,1,128]{2,1,0:T(1,128)S(1)}, f32[32,64,128]{2,1,0:T(8,128)S(1)}, f32[32,64,64]{2,1,0:T(8,128)S(1)}) custom-call(s32[8,32]{1,0:T(8,128)S(1)} %get-tuple-element.25.near_src, s32[32]{0:T(128)S(1)} %get-tuple-element.26.count_src, s32[8,32]{1,0:T(8,128)S(1)} %get-tuple-element.27.far_src, f32[32,8,128]{2,1,0:T(8,128)S(1)} %get-tuple-element.28.pack, ...), custom_call_target="tpu_custom_call" | custom-call | flops 200000000 | bytes 65536 | tf_op jit(solution)/shard_map/pallas_call | solution.py:475
  51.6 0.0 all-to-all-done.1.refs_1_
  51.6 3.6 %shard_map.94 = f32[32,128]{1,0:T(8,128)} custom-call(f32[40,1,128]{2,1,0:T(1,128)S(1)} %all_to_all.10.refs_0_, f32[192,1,128]{2,1,0:T(1,128)S(1)} %all-to-all-done.1.refs_1_, f32[27,1,64]{2,1,0:T(1,128)S(1)} %get-tuple-element.23.refs_2_, f32[9,64,64]{2,1,0:T(8,128)S(1)} %get-tuple-element.24.refs_3_, f32[32,1,128]{2,1,0:T(1,128)S(1)} %get-tuple-element.32.refs_4_, ...), custom_call_target="tpu_custom_call" | custom-call | tf_op jit(solution)/shard_map/pallas_call | solution.py:459
Async XLA Ops:
  11.0 40.6 %all-to-all-start.1 = ((f32[192,1,128]{2,1,0:T(1,128)}), f32[192,1,128]{2,1,0:T(1,128)S(1)}, u32[]{:S(2)}, u32[]{:S(2)}) async-start(f32[192,1,128]{2,1,0:T(1,128)} %get-tuple-element.22), calls=%async_computation.1 | async-start | bytes 196608 | tf_op jit(solution)/shard_map/all_to_all | solution.py:453
  26.4 7.6 %collective-permute-start = (f32[8,8,128]{2,1,0:T(8,128)S(1)}, f32[8,8,128]{2,1,0:T(8,128)S(1)}, u32[]{:S(2)}, u32[]{:S(2)}) collective-permute-start(f32[8,8,128]{2,1,0:T(8,128)S(1)} %get-tuple-element.29), channel_id=1, source_target_pairs={{0,1},{1,2},{2,3},{3,4},{4,5},{5,6},{6,7},{7,8},{8,9},{9,10},{10,1... | collective-permute-start | bytes 98312 | tf_op jit(solution)/shard_map/ppermute | solution.py:447
  32.1 9.5 %collective-permute-start.1 = (f32[8,8,128]{2,1,0:T(8,128)S(1)}, f32[8,8,128]{2,1,0:T(8,128)S(1)}, u32[]{:S(2)}, u32[]{:S(2)}) collective-permute-start(f32[8,8,128]{2,1,0:T(8,128)S(1)} %get-tuple-element.30), channel_id=1, source_target_pairs={{1,0},{2,1},{3,2},{4,3},{5,4},{6,5},{7,6},{8,7},{9,8},{10,9},{11,1... | collective-permute-start | bytes 98312 | tf_op jit(solution)/shard_map/ppermute | solution.py:448

commit v3 on v2

--- a/solution.py
+++ b/solution.py
@@ -11,8 +11,8 @@
 AXES = ("gx", "gy", "gz")
 INTERPRET = False
 CHUNKS = 4
-UNROLL = 4
-FINISH = 4
+UNROLL = 8
+FINISH = 8
 
 
 class Layout:
@@ -29,6 +29,7 @@
         self.pairs = [both[i : i + 2] for i in range(0, len(both), 2)]
         self.rows_a = 2 + len(self.pairs)
         self.rows_b = 3
+        self.couples = [(k, min(k + 1, self.levels - 1)) for k in range(0, self.levels, 2)]
 
     def device(self, a, b):
         gz, core = a % self.nz, a // self.nz
@@ -67,13 +68,17 @@
     return jnp.sum(jnp.where(mask, col, 0.0), axis=0, keepdims=True)
 
 
+def product(x, y):
+    return jnp.dot(x, y, precision=lax.Precision.HIGHEST, preferred_element_type=jnp.float32)
+
+
 def side(left, right):
     return jnp.concatenate([left, right], axis=1)
 
 
 def pre_kernel(
     lay, pts_hbm, q_hbm, p_hbm, e_hbm, w_hbm, t_hbm, l1_hbm, l2_hbm, l3_hbm,
-    pack, lo, hi, send, msg, e_ref, p_ref, l1, l2, l3, pts, q, w_ref, t_ref, sem,
+    pack, lo, hi, send, msg, f_ref, p_ref, l1, l2, l3, pts, q, w_ref, t_ref, e_ref, sem,
 ):
     leaves, rank = w_ref.shape[0], w_ref.shape[1]
     step = leaves // CHUNKS
@@ -90,8 +95,8 @@
         )
         )
     ]
-    small[0].start()
-    small[1].start()
+    for copy in small[:3]:
+        copy.start()
     copies = []
     for c in range(CHUNKS):
         part = pl.ds(c * step, step)
@@ -104,7 +109,7 @@
     for w_copy, t_copy in copies:
         w_copy.start()
         t_copy.start()
-    for copy in small[2:]:
+    for copy in small[3:]:
         copy.start()
     small[0].wait()
     small[1].wait()
@@ -122,10 +127,21 @@
         for r in range(3):
             pack[i, 5 + r : 6 + r, :] = twice[r][i : i + 1, :]
 
+    assert lay.levels <= 2 * CHUNKS + 1
     total = jnp.zeros((rank, rank), jnp.float32)
     for c in range(CHUNKS):
         copies[c][0].wait()
         copies[c][1].wait()
+        if c == 0:
+            small[2].wait()
+            f_ref[0] = e_ref[0]
+            doubles = {k: product(e_ref[k], e_ref[k + 1]) for k in range(0, lay.levels - 2, 2)}
+            if doubles:
+                f_ref[1] = doubles[0]
+        else:
+            for k in (2 * c, 2 * c + 1):
+                if k < lay.levels - 1:
+                    f_ref[k] = product(f_ref[2 * c - 1], doubles[k - 1] if k % 2 else e_ref[k])
         for i in range(c * step, (c + 1) * step):
             own = jnp.where(mask, charge[i : i + 1, :rank], 0.0)
             col = jnp.sum(w_ref[i] * other[i : i + 1, :rank] + own, axis=1, keepdims=True)
@@ -133,15 +149,13 @@
             pack[i, 4:5, :] = to_row(col, mask2)
     lo[...] = pack[0:HALO]
     hi[...] = pack[leaves - HALO : leaves]
-    for copy in small[2:]:
+    for copy in small[3:]:
         copy.wait()
 
     rows = [jnp.sum(total, axis=0, keepdims=True)]
-    for k in range(0, lay.levels - 1, 2):
-        col = jnp.sum(jnp.transpose(e_ref[k]) * rows[k], axis=1, keepdims=True)
-        rows.append(to_row(col, mask))
-        if k + 2 < lay.levels:
-            rows.append(jnp.sum(e_ref[k + 1] * col, axis=0, keepdims=True))
+    col = jnp.sum(jnp.where(mask, rows[0], 0.0), axis=1, keepdims=True)
+    for k in range(1, lay.levels):
+        rows.append(jnp.sum(f_ref[k - 1] * col, axis=0, keepdims=True))
 
     head = [side(rows[k], p_ref[3 * k]) for k in range(lay.levels)]
     tail = [side(p_ref[3 * k + 1], p_ref[3 * k + 2]) for k in range(lay.levels)]
@@ -191,8 +205,8 @@
 
 
 def near_kernel(
-    near_src, count_src, far_src, pack, lo, hi, after, t_hbm, w_hbm,
-    near_out, far_out, w_out, near_list, near_count, far_list, win, tgt, acc, t_ref, sem,
+    lay, near_src, count_src, far_src, pack, lo, hi, after, p_ref, t_hbm, w_hbm,
+    near_out, far_out, w_out, node_out, p_s, near_list, near_count, far_list, win, tgt, acc, t_ref, sem,
 ):
     del after
     copies = [
@@ -228,14 +242,23 @@
         rest = x - high
         mid = rest.astype(jnp.bfloat16).astype(jnp.float32)
         parts = jnp.concatenate([high, mid, rest - mid, jnp.zeros_like(x)], axis=0)
-        cols = jnp.transpose(parts).astype(jnp.bfloat16)
-        out = jnp.dot(cols, choose, preferred_element_type=jnp.float32)
+        out = lax.dot_general(
+            parts.astype(jnp.bfloat16), choose, (((0,), (0,)), ((), ())), preferred_element_type=jnp.float32
+        )
         return [out[:, c * lanes : (c + 1) * lanes] for c in range(3)]
 
     def keep(i, cols):
         for c in range(3):
             tgt[i, c] = cols[c]
 
+    for k in range(3 * lay.levels):
+        p_s[k : k + 1, :] = p_ref[k]
+    own = jnp.transpose(p_s[...])
+    half = lax.broadcasted_iota(jnp.int32, (rank, lanes), 1) < rank
+    for n, (one, two) in enumerate(lay.couples):
+        for c in range(3):
+            left, right = own[:, 3 * one + c : 3 * one + c + 1], own[:, 3 * two + c : 3 * two + c + 1]
+            node_out[3 * n + c] = jnp.where(half, left, right)
     for i in range(UNROLL):
         keep(i, spread(i))
     for copy in copies[:3]:
@@ -309,15 +332,12 @@
     copies[4].wait()
 
 
-def post_kernel(lay, recv_a, recv_b, p_ref, e_ref, near, far, w_ref, out, p_s, row_s, up_s):
+def post_kernel(lay, recv_a, recv_b, f_ref, near, far, w_ref, node, out, row_s, up_s):
     leaves, rank = w_ref.shape[0], w_ref.shape[1]
     mask = eye(rank, rank)
     a, b = lay.place()
     got_a = lambda diff, r: recv_a[(a ^ diff) * lay.rows_a + r]
     got_b = lambda diff, r: recv_b[(b ^ diff) * lay.rows_b + r]
-    for k in range(3 * lay.levels):
-        p_s[k : k + 1, :] = p_ref[k]
-    own = jnp.transpose(p_s[...])
 
     weight, first = {}, {}
     for diff in range(1, lay.na):
@@ -335,28 +355,31 @@
         if diff < lay.ny:
             weight[lay.core] = weight[lay.core] + got_b(diff, 2)
 
-    coupling = []
-    for k in range(lay.levels):
-        top, bottom = first[k]
-        xs = [top[:, rank:], bottom[:, :rank], bottom[:, rank:]]
+    lane = lax.broadcasted_iota(jnp.int32, (1, 2 * rank), 1)
+    turned = lambda x: pltpu.roll(x, rank, 1)
+    value, carried = 0.0, 0.0
+    for n, (one, two) in enumerate(lay.couples):
+        (top, bottom), (top2, bottom2) = first[one], first[two]
+        xs = [
+            jnp.where(lane < rank, turned(top), top2),
+            jnp.where(lane < rank, bottom, turned(bottom2)),
+            jnp.where(lane < rank, turned(bottom), bottom2),
+        ]
+        amount = jnp.where(lane < rank, weight[one], turned(weight[two]))
         squares = 0.0
         for c in range(3):
-            d = own[:, 3 * k + c : 3 * k + c + 1] - xs[c]
+            d = node[3 * n + c] - xs[c]
             squares = squares + d * d
-        coupling.append(
-            jnp.sum(lax.rsqrt(squares + SOFTENING) * weight[k][:, :rank], axis=1, keepdims=True)
-        )
-
-    value, is_col = coupling[-1], True
-    for k in range(lay.levels - 2, -1, -1):
-        if is_col:
-            value = jnp.sum(jnp.transpose(e_ref[k]) * value, axis=0, keepdims=True) + to_row(coupling[k], mask)
-        else:
-            value = jnp.sum(e_ref[k] * value, axis=1, keepdims=True) + coupling[k]
-        is_col = not is_col
-    row = to_row(value, eye(rank, 2 * rank)) if is_col else side(value, value)
-    lane = lax.broadcasted_iota(jnp.int32, (1, 2 * rank), 1)
-    row = jnp.where(lane < rank, row, 1.0)
+        terms = lax.rsqrt(squares + SOFTENING) * amount
+        for k in (one,) if one == two else (one, two):
+            keep = lane < rank if k == one else lane >= rank
+            col = jnp.sum(jnp.where(keep, terms, 0.0), axis=1, keepdims=True)
+            if k:
+                carried = carried + f_ref[k - 1] * to_row(col, mask)
+            else:
+                value = col
+    value = value + jnp.sum(carried, axis=1, keepdims=True)
+    row = jnp.where(lane < rank, to_row(value, eye(rank, 2 * rank)), 1.0)
 
     for i in range(leaves):
         col = jnp.sum(far[i] * row, axis=1, keepdims=True)
@@ -396,6 +419,17 @@
 VM = pl.BlockSpec(memory_space=pltpu.VMEM)
 SM = pl.BlockSpec(memory_space=pltpu.SMEM)
 HB = pl.BlockSpec(memory_space=pl.ANY if INTERPRET else pltpu.HBM)
+
+
+def POST_IN():
+    return [VM] * 7
+
+
+def POST_SCRATCH(leaves, rank):
+    return [
+        pltpu.VMEM((leaves, rank), jnp.float32),
+        pltpu.VMEM((leaves, rank), jnp.float32),
+    ]
 
 
 def on_device(
@@ -419,7 +453,40 @@
     tables = (near_list.T, near_count, far_list.T)
     vec = lambda n: made((n, 1, lanes))
 
-    pack, lo, hi, send, msg, e_ref, p_ref, *lists = call(
+    pack, lo, hi, send, msg, f_ref, p_ref, *lists = call_pre(
+        lay, pts, charges, centres, transfers, interpolant, leaf_transfer, tables
+    )
+
+    recv_a = lax.all_to_all(send, AXES, 0, 0, axis_index_groups=lay.groups_a(), tiled=True)
+    count = lay.na * lay.nb
+    up = [(i, i + 1) for i in range(count - 1)]
+    low = lax.ppermute(hi, AXES, up)
+    high = lax.ppermute(lo, AXES, [(b, a) for a, b in up])
+
+    send_b, token = call(
+        lambda *refs: mid_kernel(lay, *refs), [VM, VM], [vec(lay.nb * lay.rows_b), vec(1)], []
+    )(in_vmem(recv_a), in_vmem(msg))
+    recv_b = lax.all_to_all(send_b, AXES, 0, 0, axis_index_groups=lay.groups_b(), tiled=True)
+
+    near, far, w_ref, node = near_call(
+        lay, *lists, pack, low, high, token, p_ref, leaf_transfer, interpolant
+    )
+
+    (out,) = call(
+        lambda *refs: post_kernel(lay, *refs),
+        POST_IN(),
+        [jax.ShapeDtypeStruct((leaves, lanes), jnp.float32)],
+        POST_SCRATCH(leaves, rank),
+    )(*(in_vmem(x) for x in (recv_a, recv_b, f_ref, near, far, w_ref, node)))
+    return out
+
+
+def call_pre(lay, pts, charges, centres, transfers, interpolant, leaf_transfer, tables):
+    leaves, rank = interpolant.shape[0], interpolant.shape[1]
+    lanes = charges.shape[1]
+    levels = lay.levels
+    vec = lambda n: made((n, 1, lanes))
+    return call(
         lambda *refs: pre_kernel(lay, *refs),
         [HB] * 9,
         [
@@ -428,7 +495,7 @@
             made((HALO, 8, lanes)),
             vec(lay.na * lay.rows_a),
             vec(2 * levels),
-            made((levels, rank, rank)),
+            made((levels - 1, rank, rank)),
             made((3 * levels, 1, rank)),
             *(made(x.shape, jnp.int32) for x in tables),
         ],
@@ -437,46 +504,26 @@
             pltpu.VMEM((leaves, lanes), jnp.float32),
             pltpu.VMEM((leaves, rank, rank), jnp.float32),
             pltpu.VMEM((leaves, rank, rank), jnp.float32),
+            pltpu.VMEM((levels, rank, rank), jnp.float32),
             pltpu.SemaphoreType.DMA((2 * CHUNKS + 7,)),
         ],
     )(*(in_hbm(x) for x in (pts, charges, centres, transfers, interpolant, leaf_transfer, *tables)))
 
-    recv_a = lax.all_to_all(send, AXES, 0, 0, axis_index_groups=lay.groups_a(), tiled=True)
-    count = lay.na * lay.nb
-    up = [(i, i + 1) for i in range(count - 1)]
-    low = lax.ppermute(hi, AXES, up)
-    high = lax.ppermute(lo, AXES, [(b, a) for a, b in up])
-
-    send_b, token = call(
-        lambda *refs: mid_kernel(lay, *refs), [VM, VM], [vec(lay.nb * lay.rows_b), vec(1)], []
-    )(in_vmem(recv_a), in_vmem(msg))
-    recv_b = lax.all_to_all(send_b, AXES, 0, 0, axis_index_groups=lay.groups_b(), tiled=True)
-
-    near, far, w_ref = near_call(
-        *lists, pack, low, high, token, leaf_transfer, interpolant
-    )
-
-    (out,) = call(
-        lambda *refs: post_kernel(lay, *refs),
-        [VM] * 7,
-        [jax.ShapeDtypeStruct((leaves, lanes), jnp.float32)],
-        [
-            pltpu.VMEM((-(-3 * levels // 8) * 8, rank), jnp.float32),
-            pltpu.VMEM((leaves, rank), jnp.float32),
-            pltpu.VMEM((leaves, rank), jnp.float32),
-        ],
-    )(*(in_vmem(x) for x in (recv_a, recv_b, p_ref, e_ref, near, far, w_ref)))
-    return out
-
-
-def near_call(near_list, near_count, far_list, pack, low, high, token, leaf_transfer, interpolant):
+
+def near_call(lay, near_list, near_count, far_list, pack, low, high, token, p_ref, leaf_transfer, interpolant):
     leaves, rank = interpolant.shape[0], interpolant.shape[1]
     lanes = pack.shape[2]
     return call(
-        near_kernel,
-        [VM] * 7 + [HB] * 2,
-        [made((leaves, 1, lanes)), made((leaves, rank, lanes)), made((leaves, rank, rank))],
+        lambda *refs: near_kernel(lay, *refs),
+        [VM] * 8 + [HB] * 2,
         [
+            made((leaves, 1, lanes)),
+            made((leaves, rank, lanes)),
+            made((leaves, rank, rank)),
+            made((3 * len(lay.couples), rank, lanes)),
+        ],
+        [
+            pltpu.VMEM((-(-3 * lay.levels // 8) * 8, rank), jnp.float32),
             pltpu.SMEM(near_list.shape, jnp.int32),
             pltpu.SMEM(near_count.shape, jnp.int32),
             pltpu.SMEM(far_list.shape, jnp.int32),
@@ -488,7 +535,7 @@
         ],
         flops=200_000_000,
     )(
-        *(in_vmem(x) for x in (near_list, near_count, far_list, pack, low, high, token)),
+        *(in_vmem(x) for x in (near_list, near_count, far_list, pack, low, high, token, p_ref)),
         *(in_hbm(x) for x in (leaf_transfer, interpolant)),
     )
 

time: 55.6 us -> 52.4 us (0.942)
  Pallas kernels: 16.9 us -> 13.7 us
    pallas_call x3, Pallas kernels: 16.1 us -> 13 us  [the longest x1 8.99 us: near_call(): call(lambda *refs: near_kernel(lay, *refs), [VM] * 8 + [HB] * 2, [made((l...]
  transfers between devices with their start and end apart: 3 -> 3, of which waited for: 1 -> 1; matrix products, arithmetic and copies ran while one was open for 0% -> 0% of each run, Pallas kernels for 18% -> 17%
where the time goes in v3:
time: 52.4 us; the launch traced here: 52.1 us
  starting transfers between devices  22.9 us (44%)
  Pallas kernels  13.7 us (26%)
  blocking collectives  7.84 us (15%)
  waiting for transfers between devices  7.52 us (14%)
    all_to_all x1, starting transfers between devices, on_device(): lax.all_to_all(send_b, AXES, 0, 0, axis_index_groups=lay.groups_b(), tile...  15.3 us
    pallas_call x1, Pallas kernels, near_call(): call(lambda *refs: near_kernel(lay, *refs), [VM] * 8 + [HB] * 2, [made((l...  8.99 us
    all_to_all x1, blocking collectives, on_device(): lax.all_to_all(send, AXES, 0, 0, axis_index_groups=lay.groups_a(), tiled=...  7.84 us
    ppermute x1, waiting for transfers between devices, on_device(): high = lax.ppermute(lo, AXES, [(b, a) for a, b in up])  7.51 us
    ppermute x1, starting transfers between devices, on_device(): low = lax.ppermute(hi, AXES, up)  5.68 us
    pallas_call x1, Pallas kernels, call_pre(): call(lambda *refs: pre_kernel(lay, *refs), [HB] * 9, [made((leaves, 8, la...  2.38 us
    ppermute x1, starting transfers between devices, on_device(): high = lax.ppermute(lo, AXES, [(b, a) for a, b in up])  1.92 us
    pallas_call x1, Pallas kernels, on_device(): call(lambda *refs: post_kernel(lay, *refs), POST_IN(), [jax.ShapeDtypeStr...  1.6 us
  transfers between devices with their start and end apart: 3, of which 1 were waited for; matrix products, arithmetic and copies ran while one was open for 0% of the time, Pallas kernels for 17%

profile of v3, /device:TPU:63, one launch (start us, length us, event | category | flops | bytes accessed | tf_op | source)
XLA Modules:
  0.0 52.1 jit_solution(15104658437513144096)
XLA Ops:
  0.0 2.4 %shard_map.91 = (f32[32,8,128]{2,1,0:T(8,128)S(1)}, f32[8,8,128]{2,1,0:T(8,128)S(1)}, f32[8,8,128]{2,1,0:T(8,128)S(1)}, f32[40,1,128]{2,1,0:T(1,128)S(1)}, f32[1...) custom-call(f32[3,32,128]{2,1,0:T(8,128)} %bitcast.6, ...), custom_call_target="tpu_custom_call" | custom-call | tf_op jit(solution)/shard_map/pallas_call | solution.py:489
  2.4 7.8 %all_to_all.10.refs_0_ = f32[40,1,128]{2,1,0:T(1,128)S(1)} all-to-all(f32[40,1,128]{2,1,0:T(1,128)S(1)} %get-tuple-element.21), channel_id=1, replica_groups={{0,1,2,3,32,33,34,35},{4,5,6,7,36,37,38,39},{8,9,10,11,40,41,42,43},{12..., dimensions={0} | all-to-all | bytes 40960 | tf_op jit(solution)/shard_map/all_to_all | solution.py:460
  10.2 0.8 %shard_map.92 = (f32[192,1,128]{2,1,0:T(1,128)}, f32[1,1,128]{2,1,0:T(1,128)S(1)}) custom-call(f32[40,1,128]{2,1,0:T(1,128)S(1)} %all_to_all.10.refs_0_, f32[18,1,128]{2,1,0:T(1,128)S(1)} %get-tuple-element.22.refs_1_), custom_call_target="tpu_custom_call" | custom-call | tf_op jit(solution)/shard_map/pallas_call | solution.py:466
  11.0 15.3 %all-to-all-start.1 = ((f32[192,1,128]{2,1,0:T(1,128)}), f32[192,1,128]{2,1,0:T(1,128)S(1)}, u32[]{:S(2)}, u32[]{:S(2)}) async-start(f32[192,1,128]{2,1,0:T(1,128)} %get-tuple-element.23), calls=%async_computation.1 | async-start | bytes 196608 | tf_op jit(solution)/shard_map/all_to_all | solution.py:469
  26.4 5.7 %collective-permute-start = (f32[8,8,128]{2,1,0:T(8,128)S(1)}, f32[8,8,128]{2,1,0:T(8,128)S(1)}, u32[]{:S(2)}, u32[]{:S(2)}) collective-permute-start(f32[8,8,128]{2,1,0:T(8,128)S(1)} %get-tuple-element.29), channel_id=1, source_target_pairs={{0,1},{1,2},{2,3},{3,4},{4,5},{5,6},{6,7},{7,8},{8,9},{9,10},{10,1... | collective-permute-start | bytes 98312 | tf_op jit(solution)/shard_map/ppermute | solution.py:463
  32.0 1.9 %collective-permute-start.1 = (f32[8,8,128]{2,1,0:T(8,128)S(1)}, f32[8,8,128]{2,1,0:T(8,128)S(1)}, u32[]{:S(2)}, u32[]{:S(2)}) collective-permute-start(f32[8,8,128]{2,1,0:T(8,128)S(1)} %get-tuple-element.30), channel_id=1, source_target_pairs={{1,0},{2,1},{3,2},{4,3},{5,4},{6,5},{7,6},{8,7},{9,8},{10,9},{11,1... | collective-permute-start | bytes 98312 | tf_op jit(solution)/shard_map/ppermute | solution.py:464
  34.0 0.0 collective-permute-done.refs_4_
  34.0 7.5 %collective-permute-done.1.refs_5_ = f32[8,8,128]{2,1,0:T(8,128)S(1)} collective-permute-done((f32[8,8,128]{2,1,0:T(8,128)S(1)}, f32[8,8,128]{2,1,0:T(8,128)S(1)}, u32[]{:S(2)}, u32[]{:S(2)}) %collective-permute-start.1) | collective-permute-done | bytes 32800 | tf_op jit(solution)/shard_map/ppermute | solution.py:464
  41.5 9.0 %shard_map.93 = (f32[32,1,128]{2,1,0:T(1,128)S(1)}, f32[32,64,128]{2,1,0:T(8,128)S(1)}, f32[32,64,64]{2,1,0:T(8,128)S(1)}, f32[15,64,128]{2,1,0:T(8,128)S(1)}) custom-call(s32[8,32]{1,0:T(8,128)S(1)} %get-tuple-element.25.refs_0_, s32[32]{0:T(128)S(1)} %get-tuple-element.26.refs_1_, s32[8,32]{1,0:T(8,128)S(1)} %get-tuple-element.27.refs_2_, ...), custom_call_target="tpu_custom_call" | custom-call | flops 200000000 | bytes 65536 | tf_op jit(solution)/shard_map/pallas_call | solution.py:516
  50.5 0.0 all-to-all-done.1.refs_1_
  50.5 1.6 %shard_map.94 = f32[32,128]{1,0:T(8,128)} custom-call(f32[40,1,128]{2,1,0:T(1,128)S(1)} %all_to_all.10.refs_0_, f32[192,1,128]{2,1,0:T(1,128)S(1)} %all-to-all-done.1.refs_1_, f32[8,64,64]{2,1,0:T(8,128)S(1)} %get-tuple-element.24.refs_2_, f32[32,1,128]{2,1,0:T(1,128)S(1)} %get-tuple-element.33.refs_3_, f32[32,64,128]{2,1,0:T(8,128)S(1)} %get-tuple-element.34.refs_4_, ...), custom_call_target="tpu_custom_call" | custom-call | tf_op jit(solution)/shard_map/pallas_call | solution.py:475
Async XLA Ops:
  11.0 39.5 %all-to-all-start.1 = ((f32[192,1,128]{2,1,0:T(1,128)}), f32[192,1,128]{2,1,0:T(1,128)S(1)}, u32[]{:S(2)}, u32[]{:S(2)}) async-start(f32[192,1,128]{2,1,0:T(1,128)} %get-tuple-element.23), calls=%async_computation.1 | async-start | bytes 196608 | tf_op jit(solution)/shard_map/all_to_all | solution.py:469
  26.4 7.6 %collective-permute-start = (f32[8,8,128]{2,1,0:T(8,128)S(1)}, f32[8,8,128]{2,1,0:T(8,128)S(1)}, u32[]{:S(2)}, u32[]{:S(2)}) collective-permute-start(f32[8,8,128]{2,1,0:T(8,128)S(1)} %get-tuple-element.29), channel_id=1, source_target_pairs={{0,1},{1,2},{2,3},{3,4},{4,5},{5,6},{6,7},{7,8},{8,9},{9,10},{10,1... | collective-permute-start | bytes 98312 | tf_op jit(solution)/shard_map/ppermute | solution.py:463
  32.0 9.5 %collective-permute-start.1 = (f32[8,8,128]{2,1,0:T(8,128)S(1)}, f32[8,8,128]{2,1,0:T(8,128)S(1)}, u32[]{:S(2)}, u32[]{:S(2)}) collective-permute-start(f32[8,8,128]{2,1,0:T(8,128)S(1)} %get-tuple-element.30), channel_id=1, source_target_pairs={{1,0},{2,1},{3,2},{4,3},{5,4},{6,5},{7,6},{8,7},{9,8},{10,9},{11,1... | collective-permute-start | bytes 98312 | tf_op jit(solution)/shard_map/ppermute | solution.py:464

commit v4 on v3

--- a/solution.py
+++ b/solution.py
@@ -204,32 +204,37 @@
     token[0] = core
 
 
-def near_kernel(
-    lay, near_src, count_src, far_src, pack, lo, hi, after, p_ref, t_hbm, w_hbm,
-    near_out, far_out, w_out, node_out, p_s, near_list, near_count, far_list, win, tgt, acc, t_ref, sem,
-):
+def near_kernel(lay, start, near_src, count_src, far_src, pack, halo, after, *refs):
     del after
-    copies = [
-        pltpu.make_async_copy(src, dst, sem.at[n])
-        for n, (src, dst) in enumerate(
-            (
-                (near_src, near_list),
-                (count_src, near_count),
-                (far_src, far_list),
-                (t_hbm, t_ref),
-                (w_hbm, w_out),
-            )
-        )
-    ]
-    for copy in copies:
-        copy.start()
-    leaves, lanes = pack.shape[0], pack.shape[2]
+    head = start == 0
+    if head:
+        p_ref, t_hbm, w_hbm, near_out, far_out, w_out, node_out, p_s = refs[:8]
+        refs = refs[8:]
+    else:
+        t_hbm, near_out, far_out = refs[:3]
+        refs = refs[3:]
+    near_list, near_count, far_list, win, tgt, acc, t_ref, sem = refs
+    leaves, lanes = near_out.shape[0], pack.shape[2]
     rank = lanes // 2
     tiles = lanes // 8
     far_tiles = rank // 8
-    win[0:HALO] = lo[...]
-    win[HALO : HALO + leaves] = pack[...]
-    win[HALO + leaves :] = hi[...]
+    moves = [
+        (near_src, near_list),
+        (count_src, near_count),
+        (far_src, far_list),
+        (t_hbm.at[pl.ds(start, leaves)], t_ref),
+    ]
+    if head:
+        moves.append((w_hbm, w_out))
+    copies = [pltpu.make_async_copy(src, dst, sem.at[n]) for n, (src, dst) in enumerate(moves)]
+    for copy in copies:
+        copy.start()
+    total = pack.shape[0]
+    if head:
+        win[0:HALO] = halo[...]
+    else:
+        win[HALO + total :] = halo[...]
+    win[HALO : HALO + total] = pack[...]
 
     pick = lax.broadcasted_iota(jnp.int32, (32, 3 * lanes), 0) % 8
     wide = lax.broadcasted_iota(jnp.int32, (32, 3 * lanes), 1) // lanes
@@ -237,7 +242,7 @@
     used = lax.broadcasted_iota(jnp.int32, (8, lanes), 0) < 3
 
     def spread(i):
-        x = jnp.where(used, win[HALO + i], 0.0)
+        x = jnp.where(used, win[HALO + start + i], 0.0)
         high = x.astype(jnp.bfloat16).astype(jnp.float32)
         rest = x - high
         mid = rest.astype(jnp.bfloat16).astype(jnp.float32)
@@ -251,14 +256,15 @@
         for c in range(3):
             tgt[i, c] = cols[c]
 
-    for k in range(3 * lay.levels):
-        p_s[k : k + 1, :] = p_ref[k]
-    own = jnp.transpose(p_s[...])
-    half = lax.broadcasted_iota(jnp.int32, (rank, lanes), 1) < rank
-    for n, (one, two) in enumerate(lay.couples):
-        for c in range(3):
-            left, right = own[:, 3 * one + c : 3 * one + c + 1], own[:, 3 * two + c : 3 * two + c + 1]
-            node_out[3 * n + c] = jnp.where(half, left, right)
+    if head:
+        for k in range(3 * lay.levels):
+            p_s[k : k + 1, :] = p_ref[k]
+        own = jnp.transpose(p_s[...])
+        half = lax.broadcasted_iota(jnp.int32, (rank, lanes), 1) < rank
+        for n, (one, two) in enumerate(lay.couples):
+            for c in range(3):
+                left, right = own[:, 3 * one + c : 3 * one + c + 1], own[:, 3 * two + c : 3 * two + c + 1]
+                node_out[3 * n + c] = jnp.where(half, left, right)
     for i in range(UNROLL):
         keep(i, spread(i))
     for copy in copies[:3]:
@@ -276,36 +282,40 @@
 
     lane = lax.broadcasted_iota(jnp.int32, (8, lanes), 1)
 
-    def far_field(g, carry):
-        ahead = [spread((g + 1) * UNROLL + u) for u in range(UNROLL)]
+    def far_field(g, more):
+        ahead = [spread((g + 1) * UNROLL + u) for u in range(UNROLL)] if more else []
         for u in range(UNROLL):
             i = g * UNROLL + u
             both = []
             for m in range(0, far_list.shape[0], 2):
-                block = jnp.where(lane < rank, win[far_list[m, i]], win[far_list[m + 1, i]])
+                block = jnp.where(lane < rank, win[far_list[m, start + i]], win[far_list[m + 1, start + i]])
                 both.append([jnp.broadcast_to(block[r : r + 1, :], (8, lanes)) for r in (5, 6, 7, 4)])
             for t in range(far_tiles):
                 far = weighted(i, t, both[0])
                 for xs in both[1:]:
                     far = far + weighted(i, t, xs)
                 far_out[i, pl.ds(8 * t, 8), :] = far + pltpu.roll(far, rank, 1)
-        for u in range(UNROLL):
-            i = (g + 1) * UNROLL + u
-            keep(i, ahead[u])
+        for u, cols in enumerate(ahead):
+            keep((g + 1) * UNROLL + u, cols)
+
+    def far_step(g, carry):
+        far_field(g, True)
         return carry
 
-    lax.fori_loop(0, leaves // UNROLL, far_field, 0)
+    groups = leaves // UNROLL
+    lax.fori_loop(0, groups - 1, far_step, 0)
+    far_field(groups - 1, False)
 
     def leaf(i, carry):
-        count = near_count[i]
+        count = near_count[start + i]
         for t in range(tiles):
             acc[i, pl.ds(8 * t, 8), :] = jnp.zeros((8, lanes), jnp.float32)
 
         def slots(n, inner):
             m = 2 * n + 1
-            one = rows(near_list[m, i], range(4))
+            one = rows(near_list[m, start + i], range(4))
             then = jnp.minimum(m + 1, near_list.shape[0] - 1)
-            two = rows(near_list[then, i], range(4))
+            two = rows(near_list[then, start + i], range(4))
             two[3] = two[3] * jnp.where(m + 1 < count, 1.0, 0.0)
             for t in range(tiles):
                 at = pl.ds(8 * t, 8)
@@ -318,7 +328,7 @@
     copies[3].wait()
 
     def finish(i, carry):
-        own = rows(near_list[0, i], range(4))
+        own = rows(near_list[0, start + i], range(4))
         sums = [acc[i, pl.ds(8 * t, 8), :] + weighted(i, t, own) for t in range(tiles)]
         whole = jnp.concatenate(sums, axis=0)
         near_out[i] = jnp.sum(jnp.transpose(whole), axis=0, keepdims=True)
@@ -329,10 +339,11 @@
         return carry
 
     lax.fori_loop(0, leaves, finish, 0, unroll=FINISH)
-    copies[4].wait()
-
-
-def post_kernel(lay, recv_a, recv_b, f_ref, near, far, w_ref, node, out, row_s, up_s):
+    for copy in copies[4:]:
+        copy.wait()
+
+
+def post_kernel(lay, recv_a, recv_b, f_ref, near, far, near2, far2, w_ref, node, out, row_s, up_s):
     leaves, rank = w_ref.shape[0], w_ref.shape[1]
     mask = eye(rank, rank)
     a, b = lay.place()
@@ -381,12 +392,14 @@
     value = value + jnp.sum(carried, axis=1, keepdims=True)
     row = jnp.where(lane < rank, to_row(value, eye(rank, 2 * rank)), 1.0)
 
+    split = far.shape[0]
     for i in range(leaves):
-        col = jnp.sum(far[i] * row, axis=1, keepdims=True)
+        sums = far[i] if i < split else far2[i - split]
+        col = jnp.sum(sums * row, axis=1, keepdims=True)
         row_s[i : i + 1, :] = to_row(col, mask)
         up_s[i : i + 1, :] = jnp.sum(w_ref[i] * col, axis=0, keepdims=True)
     for i in range(leaves):
-        out[i : i + 1, :] = near[i]
+        out[i : i + 1, :] = near[i] if i < split else near2[i - split]
     out[...] = out[...] + side(row_s[...], up_s[...])
 
 
@@ -422,7 +435,7 @@
 
 
 def POST_IN():
-    return [VM] * 7
+    return [VM] * 9
 
 
 def POST_SCRATCH(leaves, rank):
@@ -468,16 +481,18 @@
     )(in_vmem(recv_a), in_vmem(msg))
     recv_b = lax.all_to_all(send_b, AXES, 0, 0, axis_index_groups=lay.groups_b(), tiled=True)
 
+    split = leaves - HALO
     near, far, w_ref, node = near_call(
-        lay, *lists, pack, low, high, token, p_ref, leaf_transfer, interpolant
+        lay, 0, split, lists, pack, low, token, p_ref, leaf_transfer, interpolant
     )
+    near2, far2 = near_call(lay, split, HALO, lists, pack, high, near, p_ref, leaf_transfer, interpolant)
 
     (out,) = call(
         lambda *refs: post_kernel(lay, *refs),
         POST_IN(),
         [jax.ShapeDtypeStruct((leaves, lanes), jnp.float32)],
         POST_SCRATCH(leaves, rank),
-    )(*(in_vmem(x) for x in (recv_a, recv_b, f_ref, near, far, w_ref, node)))
+    )(*(in_vmem(x) for x in (recv_a, recv_b, f_ref, near, far, near2, far2, w_ref, node)))
     return out
 
 
@@ -510,34 +525,32 @@
     )(*(in_hbm(x) for x in (pts, charges, centres, transfers, interpolant, leaf_transfer, *tables)))
 
 
-def near_call(lay, near_list, near_count, far_list, pack, low, high, token, p_ref, leaf_transfer, interpolant):
-    leaves, rank = interpolant.shape[0], interpolant.shape[1]
+def near_call(lay, start, leaves, lists, pack, halo, token, p_ref, leaf_transfer, interpolant):
+    total, rank = interpolant.shape[0], interpolant.shape[1]
     lanes = pack.shape[2]
+    head = start == 0
+    outs = [made((leaves, 1, lanes)), made((leaves, rank, lanes))]
+    extra = []
+    if head:
+        outs += [made((total, rank, rank)), made((3 * len(lay.couples), rank, lanes))]
+        extra = [pltpu.VMEM((-(-3 * lay.levels // 8) * 8, rank), jnp.float32)]
+    near_inputs = [*lists, pack, halo, token] + ([p_ref] if head else [])
+    far_inputs = [leaf_transfer] + ([interpolant] if head else [])
     return call(
-        lambda *refs: near_kernel(lay, *refs),
-        [VM] * 8 + [HB] * 2,
+        lambda *refs: near_kernel(lay, start, *refs),
+        [VM] * len(near_inputs) + [HB] * len(far_inputs),
+        outs,
         [
-            made((leaves, 1, lanes)),
-            made((leaves, rank, lanes)),
-            made((leaves, rank, rank)),
-            made((3 * len(lay.couples), rank, lanes)),
-        ],
-        [
-            pltpu.VMEM((-(-3 * lay.levels // 8) * 8, rank), jnp.float32),
-            pltpu.SMEM(near_list.shape, jnp.int32),
-            pltpu.SMEM(near_count.shape, jnp.int32),
-            pltpu.SMEM(far_list.shape, jnp.int32),
-            pltpu.VMEM((leaves + 2 * HALO, 8, lanes), jnp.float32),
-            pltpu.VMEM((leaves + UNROLL, 3, lanes, lanes), jnp.float32),
+            *extra,
+            *(pltpu.SMEM(x.shape, jnp.int32) for x in lists),
+            pltpu.VMEM((total + 2 * HALO, 8, lanes), jnp.float32),
+            pltpu.VMEM((leaves, 3, lanes, lanes), jnp.float32),
             pltpu.VMEM((leaves, lanes, lanes), jnp.float32),
             pltpu.VMEM((leaves, rank, rank), jnp.float32),
             pltpu.SemaphoreType.DMA((5,)),
         ],
         flops=200_000_000,
-    )(
-        *(in_vmem(x) for x in (near_list, near_count, far_list, pack, low, high, token, p_ref)),
-        *(in_hbm(x) for x in (leaf_transfer, interpolant)),
-    )
+    )(*(in_vmem(x) for x in near_inputs), *(in_hbm(x) for x in far_inputs))
 
 
 def solution(mesh):

time: 52.4 us -> 50.3 us (0.960)
  the two profiles are of different devices: /device:TPU:63 before, /device:TPU:1 now
where the time goes in v4:
time: 50.3 us; the launch traced here: 50 us
  starting transfers between devices  21.6 us (43%)
  Pallas kernels  14.3 us (28%)
  blocking collectives  14.1 us (28%)
    all_to_all x1, blocking collectives, on_device(): lax.all_to_all(send, AXES, 0, 0, axis_index_groups=lay.groups_a(), tiled=...  14.1 us
    all_to_all x1, starting transfers between devices, on_device(): lax.all_to_all(send_b, AXES, 0, 0, axis_index_groups=lay.groups_b(), tile...  12.7 us
    pallas_call x2, Pallas kernels, near_call(): call(lambda *refs: near_kernel(lay, start, *refs), [VM] * len(near_inputs...  9.51 us
    ppermute x1, starting transfers between devices, on_device(): high = lax.ppermute(lo, AXES, [(b, a) for a, b in up])  6.64 us
    pallas_call x1, Pallas kernels, call_pre(): call(lambda *refs: pre_kernel(lay, *refs), [HB] * 9, [made((leaves, 8, la...  2.37 us
    ppermute x1, starting transfers between devices, on_device(): low = lax.ppermute(hi, AXES, up)  2.25 us
    pallas_call x1, Pallas kernels, on_device(): call(lambda *refs: post_kernel(lay, *refs), POST_IN(), [jax.ShapeDtypeStr...  1.6 us
  transfers between devices with their start and end apart: 3, of which 0 were waited for; matrix products, arithmetic and copies ran while one was open for 0% of the time, Pallas kernels for 19%

profile of v4, /device:TPU:1, one launch (start us, length us, event | category | flops | bytes accessed | tf_op | source)
XLA Modules:
  0.0 50.0 jit_solution(10024765152749677018)
XLA Ops:
  0.0 2.4 %shard_map.91 = (f32[32,8,128]{2,1,0:T(8,128)S(1)}, f32[8,8,128]{2,1,0:T(8,128)S(1)}, f32[8,8,128]{2,1,0:T(8,128)S(1)}, f32[40,1,128]{2,1,0:T(1,128)S(1)}, f32[1...) custom-call(f32[3,32,128]{2,1,0:T(8,128)} %bitcast.6, ...), custom_call_target="tpu_custom_call" | custom-call | tf_op jit(solution)/shard_map/pallas_call | solution.py:504
  2.4 14.1 %all_to_all.10.refs_0_ = f32[40,1,128]{2,1,0:T(1,128)S(1)} all-to-all(f32[40,1,128]{2,1,0:T(1,128)S(1)} %get-tuple-element.23), channel_id=1, replica_groups={{0,1,2,3,32,33,34,35},{4,5,6,7,36,37,38,39},{8,9,10,11,40,41,42,43},{12..., dimensions={0} | all-to-all | bytes 40960 | tf_op jit(solution)/shard_map/all_to_all | solution.py:473
  16.5 0.8 %shard_map.92 = (f32[192,1,128]{2,1,0:T(1,128)}, f32[1,1,128]{2,1,0:T(1,128)S(1)}) custom-call(f32[40,1,128]{2,1,0:T(1,128)S(1)} %all_to_all.10.refs_0_, f32[18,1,128]{2,1,0:T(1,128)S(1)} %get-tuple-element.24.refs_1_), custom_call_target="tpu_custom_call" | custom-call | tf_op jit(solution)/shard_map/pallas_call | solution.py:479
  17.3 12.7 %all-to-all-start.1 = ((f32[192,1,128]{2,1,0:T(1,128)}), f32[192,1,128]{2,1,0:T(1,128)S(1)}, u32[]{:S(2)}, u32[]{:S(2)}) async-start(f32[192,1,128]{2,1,0:T(1,128)} %get-tuple-element.25), calls=%async_computation.1 | async-start | bytes 196608 | tf_op jit(solution)/shard_map/all_to_all | solution.py:482
  30.0 2.2 %collective-permute-start = (f32[8,8,128]{2,1,0:T(8,128)S(1)}, f32[8,8,128]{2,1,0:T(8,128)S(1)}, u32[]{:S(2)}, u32[]{:S(2)}) collective-permute-start(f32[8,8,128]{2,1,0:T(8,128)S(1)} %get-tuple-element.31), channel_id=1, source_target_pairs={{0,1},{1,2},{2,3},{3,4},{4,5},{5,6},{6,7},{7,8},{8,9},{9,10},{10,1... | collective-permute-start | bytes 98312 | tf_op jit(solution)/shard_map/ppermute | solution.py:476
  32.2 6.6 %collective-permute-start.1 = (f32[8,8,128]{2,1,0:T(8,128)S(1)}, f32[8,8,128]{2,1,0:T(8,128)S(1)}, u32[]{:S(2)}, u32[]{:S(2)}) collective-permute-start(f32[8,8,128]{2,1,0:T(8,128)S(1)} %get-tuple-element.36), channel_id=1, source_target_pairs={{1,0},{2,1},{3,2},{4,3},{5,4},{6,5},{7,6},{8,7},{9,8},{10,9},{11,1... | collective-permute-start | bytes 98312 | tf_op jit(solution)/shard_map/ppermute | solution.py:477
  38.9 0.0 collective-permute-done.refs_4_
  38.9 6.9 %shard_map.93 = (f32[24,1,128]{2,1,0:T(1,128)S(1)}, f32[24,64,128]{2,1,0:T(8,128)S(1)}, f32[32,64,64]{2,1,0:T(8,128)S(1)}, f32[15,64,128]{2,1,0:T(8,128)S(1)}) custom-call(s32[8,32]{1,0:T(8,128)S(1)} %get-tuple-element.27.refs_0_, s32[32]{0:T(128)S(1)} %get-tuple-element.28.refs_1_, s32[8,32]{1,0:T(8,128)S(1)} %get-tuple-element.29.refs_2_, ...), custom_call_target="tpu_custom_call" | custom-call | flops 200000000 | bytes 65536 | tf_op jit(solution)/shard_map/pallas_call | solution.py:539
  45.8 0.0 collective-permute-done.1.refs_4_
  45.8 2.6 %shard_map.94 = (f32[8,1,128]{2,1,0:T(1,128)S(1)}, f32[8,64,128]{2,1,0:T(8,128)S(1)}) custom-call(s32[8,32]{1,0:T(8,128)S(1)} %get-tuple-element.27.refs_0_, s32[32]{0:T(128)S(1)} %get-tuple-element.28.refs_1_, s32[8,32]{1,0:T(8,128)S(1)} %get-tuple-element.29.refs_2_, f32[32,8,128]{2,1,0:T(8,128)S(1)} %get-tuple-element.30.refs_3_, ...), custom_call_target="tpu_custom_call" | custom-call | flops 200000000 | bytes 65536 | tf_op jit(solution)/shard_map/pallas_call | solution.py:539
  48.4 0.0 all-to-all-done.1.refs_1_
  48.4 1.6 %shard_map.95 = f32[32,128]{1,0:T(8,128)} custom-call(f32[40,1,128]{2,1,0:T(1,128)S(1)} %all_to_all.10.refs_0_, f32[192,1,128]{2,1,0:T(1,128)S(1)} %all-to-all-done.1.refs_1_, f32[8,64,64]{2,1,0:T(8,128)S(1)} %get-tuple-element.26.refs_2_, f32[24,1,128]{2,1,0:T(1,128)S(1)} %get-tuple-element.34.refs_5_.refs_3_, ...), custom_call_target="tpu_custom_call" | custom-call | tf_op jit(solution)/shard_map/pallas_call | solution.py:490
Async XLA Ops:
  17.3 31.2 %all-to-all-start.1 = ((f32[192,1,128]{2,1,0:T(1,128)}), f32[192,1,128]{2,1,0:T(1,128)S(1)}, u32[]{:S(2)}, u32[]{:S(2)}) async-start(f32[192,1,128]{2,1,0:T(1,128)} %get-tuple-element.25), calls=%async_computation.1 | async-start | bytes 196608 | tf_op jit(solution)/shard_map/all_to_all | solution.py:482
  30.0 8.9 %collective-permute-start = (f32[8,8,128]{2,1,0:T(8,128)S(1)}, f32[8,8,128]{2,1,0:T(8,128)S(1)}, u32[]{:S(2)}, u32[]{:S(2)}) collective-permute-start(f32[8,8,128]{2,1,0:T(8,128)S(1)} %get-tuple-element.31), channel_id=1, source_target_pairs={{0,1},{1,2},{2,3},{3,4},{4,5},{5,6},{6,7},{7,8},{8,9},{9,10},{10,1... | collective-permute-start | bytes 98312 | tf_op jit(solution)/shard_map/ppermute | solution.py:476
  32.2 13.5 %collective-permute-start.1 = (f32[8,8,128]{2,1,0:T(8,128)S(1)}, f32[8,8,128]{2,1,0:T(8,128)S(1)}, u32[]{:S(2)}, u32[]{:S(2)}) collective-permute-start(f32[8,8,128]{2,1,0:T(8,128)S(1)} %get-tuple-element.36), channel_id=1, source_target_pairs={{1,0},{2,1},{3,2},{4,3},{5,4},{6,5},{7,6},{8,7},{9,8},{10,9},{11,1... | collective-permute-start | bytes 98312 | tf_op jit(solution)/shard_map/ppermute | solution.py:477

commit v5 on v4

--- a/solution.py
+++ b/solution.py
@@ -206,7 +206,7 @@
 
 def near_kernel(lay, start, near_src, count_src, far_src, pack, halo, after, *refs):
     del after
-    head = start == 0
+    head = start == HALO
     if head:
         p_ref, t_hbm, w_hbm, near_out, far_out, w_out, node_out, p_s = refs[:8]
         refs = refs[8:]
@@ -230,9 +230,9 @@
     for copy in copies:
         copy.start()
     total = pack.shape[0]
-    if head:
+    if start == 0:
         win[0:HALO] = halo[...]
-    else:
+    elif not head:
         win[HALO + total :] = halo[...]
     win[HALO : HALO + total] = pack[...]
 
@@ -343,8 +343,8 @@
         copy.wait()
 
 
-def post_kernel(lay, recv_a, recv_b, f_ref, near, far, near2, far2, w_ref, node, out, row_s, up_s):
-    leaves, rank = w_ref.shape[0], w_ref.shape[1]
+def post_kernel(lay, recv_a, recv_b, f_ref, near1, far1, near, far, near2, far2, w_ref, node, out, row_s, up_s):
+    rank = w_ref.shape[1]
     mask = eye(rank, rank)
     a, b = lay.place()
     got_a = lambda diff, r: recv_a[(a ^ diff) * lay.rows_a + r]
@@ -392,14 +392,15 @@
     value = value + jnp.sum(carried, axis=1, keepdims=True)
     row = jnp.where(lane < rank, to_row(value, eye(rank, 2 * rank)), 1.0)
 
-    split = far.shape[0]
-    for i in range(leaves):
-        sums = far[i] if i < split else far2[i - split]
-        col = jnp.sum(sums * row, axis=1, keepdims=True)
+    where = [
+        (parts, i) for parts in ((near1, far1), (near, far), (near2, far2)) for i in range(parts[1].shape[0])
+    ]
+    for i, (parts, at) in enumerate(where):
+        col = jnp.sum(parts[1][at] * row, axis=1, keepdims=True)
         row_s[i : i + 1, :] = to_row(col, mask)
         up_s[i : i + 1, :] = jnp.sum(w_ref[i] * col, axis=0, keepdims=True)
-    for i in range(leaves):
-        out[i : i + 1, :] = near[i] if i < split else near2[i - split]
+    for i, (parts, at) in enumerate(where):
+        out[i : i + 1, :] = parts[0][at]
     out[...] = out[...] + side(row_s[...], up_s[...])
 
 
@@ -435,7 +436,7 @@
 
 
 def POST_IN():
-    return [VM] * 9
+    return [VM] * 11
 
 
 def POST_SCRATCH(leaves, rank):
@@ -471,6 +472,9 @@
     )
 
     recv_a = lax.all_to_all(send, AXES, 0, 0, axis_index_groups=lay.groups_a(), tiled=True)
+    near, far, w_ref, node = near_call(
+        lay, HALO, leaves - 2 * HALO, lists, pack, lo, hi, p_ref, leaf_transfer, interpolant
+    )
     count = lay.na * lay.nb
     up = [(i, i + 1) for i in range(count - 1)]
     low = lax.ppermute(hi, AXES, up)
@@ -481,18 +485,17 @@
     )(in_vmem(recv_a), in_vmem(msg))
     recv_b = lax.all_to_all(send_b, AXES, 0, 0, axis_index_groups=lay.groups_b(), tiled=True)
 
-    split = leaves - HALO
-    near, far, w_ref, node = near_call(
-        lay, 0, split, lists, pack, low, token, p_ref, leaf_transfer, interpolant
+    near1, far1 = near_call(lay, 0, HALO, lists, pack, low, token, p_ref, leaf_transfer, interpolant)
+    near2, far2 = near_call(
+        lay, leaves - HALO, HALO, lists, pack, high, near1, p_ref, leaf_transfer, interpolant
     )
-    near2, far2 = near_call(lay, split, HALO, lists, pack, high, near, p_ref, leaf_transfer, interpolant)
 
     (out,) = call(
         lambda *refs: post_kernel(lay, *refs),
         POST_IN(),
         [jax.ShapeDtypeStruct((leaves, lanes), jnp.float32)],
         POST_SCRATCH(leaves, rank),
-    )(*(in_vmem(x) for x in (recv_a, recv_b, f_ref, near, far, near2, far2, w_ref, node)))
+    )(*(in_vmem(x) for x in (recv_a, recv_b, f_ref, near1, far1, near, far, near2, far2, w_ref, node)))
     return out
 
 
@@ -528,7 +531,7 @@
 def near_call(lay, start, leaves, lists, pack, halo, token, p_ref, leaf_transfer, interpolant):
     total, rank = interpolant.shape[0], interpolant.shape[1]
     lanes = pack.shape[2]
-    head = start == 0
+    head = start == HALO
     outs = [made((leaves, 1, lanes)), made((leaves, rank, lanes))]
     extra = []
     if head:

time: 50.3 us -> 50.7 us (level)
    pallas_call x2 -> x3, Pallas kernels: 9.51 us -> 9.89 us  [near_call(): call(lambda *refs: near_kernel(lay, start, *refs), [VM] * len(near_inputs...]
  transfers between devices with their start and end apart: 3 -> 3, of which waited for: 0 -> 0; matrix products, arithmetic and copies ran while one was open for 0% -> 0% of each run, Pallas kernels for 19% -> 20%
where the time goes in v5:
time: 50.7 us; the launch traced here: 50.4 us
  starting transfers between devices  21.6 us (43%)
  Pallas kernels  14.6 us (29%)
  blocking collectives  14.1 us (28%)
    all_to_all x1, blocking collectives, on_device(): lax.all_to_all(send, AXES, 0, 0, axis_index_groups=lay.groups_a(), tiled=...  14.1 us
    all_to_all x1, starting transfers between devices, on_device(): lax.all_to_all(send_b, AXES, 0, 0, axis_index_groups=lay.groups_b(), tile...  12.7 us
    pallas_call x3, Pallas kernels, near_call(): call(lambda *refs: near_kernel(lay, start, *refs), [VM] * len(near_inputs...  9.89 us
    ppermute x1, starting transfers between devices, on_device(): high = lax.ppermute(lo, AXES, [(b, a) for a, b in up])  6.64 us
    pallas_call x1, Pallas kernels, call_pre(): call(lambda *refs: pre_kernel(lay, *refs), [HB] * 9, [made((leaves, 8, la...  2.38 us
    ppermute x1, starting transfers between devices, on_device(): low = lax.ppermute(hi, AXES, up)  2.25 us
    pallas_call x1, Pallas kernels, on_device(): call(lambda *refs: post_kernel(lay, *refs), POST_IN(), [jax.ShapeDtypeStr...  1.6 us
  transfers between devices with their start and end apart: 3, of which 0 were waited for; matrix products, arithmetic and copies ran while one was open for 0% of the time, Pallas kernels for 20%

profile of v5, /device:TPU:1, one launch (start us, length us, event | category | flops | bytes accessed | tf_op | source)
XLA Modules:
  0.0 50.4 jit_solution(2941165360249809131)
XLA Ops:
  0.0 2.4 %shard_map.91 = (f32[32,8,128]{2,1,0:T(8,128)S(1)}, f32[8,8,128]{2,1,0:T(8,128)S(1)}, f32[8,8,128]{2,1,0:T(8,128)S(1)}, f32[40,1,128]{2,1,0:T(1,128)S(1)}, f32[1...) custom-call(f32[3,32,128]{2,1,0:T(8,128)} %bitcast.6, ...), custom_call_target="tpu_custom_call" | custom-call | tf_op jit(solution)/shard_map/pallas_call | solution.py:507
  2.4 14.1 %all_to_all.10.refs_0_ = f32[40,1,128]{2,1,0:T(1,128)S(1)} all-to-all(f32[40,1,128]{2,1,0:T(1,128)S(1)} %get-tuple-element.25), channel_id=1, replica_groups={{0,1,2,3,32,33,34,35},{4,5,6,7,36,37,38,39},{8,9,10,11,40,41,42,43},{12..., dimensions={0} | all-to-all | bytes 40960 | tf_op jit(solution)/shard_map/all_to_all | solution.py:474
  16.5 0.8 %shard_map.92 = (f32[192,1,128]{2,1,0:T(1,128)}, f32[1,1,128]{2,1,0:T(1,128)S(1)}) custom-call(f32[40,1,128]{2,1,0:T(1,128)S(1)} %all_to_all.10.refs_0_, f32[18,1,128]{2,1,0:T(1,128)S(1)} %get-tuple-element.26.refs_1_), custom_call_target="tpu_custom_call" | custom-call | tf_op jit(solution)/shard_map/pallas_call | solution.py:483
  17.3 12.7 %all-to-all-start.1 = ((f32[192,1,128]{2,1,0:T(1,128)}), f32[192,1,128]{2,1,0:T(1,128)S(1)}, u32[]{:S(2)}, u32[]{:S(2)}) async-start(f32[192,1,128]{2,1,0:T(1,128)} %get-tuple-element.27), calls=%async_computation.1 | async-start | bytes 196608 | tf_op jit(solution)/shard_map/all_to_all | solution.py:486
  30.0 2.2 %collective-permute-start = (f32[8,8,128]{2,1,0:T(8,128)S(1)}, f32[8,8,128]{2,1,0:T(8,128)S(1)}, u32[]{:S(2)}, u32[]{:S(2)}) collective-permute-start(f32[8,8,128]{2,1,0:T(8,128)S(1)} %get-tuple-element.33.refs_5_), channel_id=1, source_target_pairs={{0,1},{1,2},{2,3},{3,4},{4,5},{5,6},{6,7},{7,8},{8,9},{9,10},{10,1... | collective-permute-start | bytes 98312 | tf_op jit(solution)/shard_map/ppermute | solution.py:480
  32.2 6.6 %collective-permute-start.1 = (f32[8,8,128]{2,1,0:T(8,128)S(1)}, f32[8,8,128]{2,1,0:T(8,128)S(1)}, u32[]{:S(2)}, u32[]{:S(2)}) collective-permute-start(f32[8,8,128]{2,1,0:T(8,128)S(1)} %get-tuple-element.37.refs_4_), channel_id=1, source_target_pairs={{1,0},{2,1},{3,2},{4,3},{5,4},{6,5},{7,6},{8,7},{9,8},{10,9},{11,1... | collective-permute-start | bytes 98312 | tf_op jit(solution)/shard_map/ppermute | solution.py:481
  38.9 4.7 %shard_map.94 = (f32[16,1,128]{2,1,0:T(1,128)S(1)}, f32[16,64,128]{2,1,0:T(8,128)S(1)}, f32[32,64,64]{2,1,0:T(8,128)S(1)}, f32[15,64,128]{2,1,0:T(8,128)S(1)}) custom-call(s32[8,32]{1,0:T(8,128)S(1)} %get-tuple-element.29.refs_0_, s32[32]{0:T(128)S(1)} %get-tuple-element.30.refs_1_, s32[8,32]{1,0:T(8,128)S(1)} %get-tuple-element.31.refs_2_, ...), custom_call_target="tpu_custom_call" | custom-call | flops 200000000 | bytes 65536 | tf_op jit(solution)/shard_map/pallas_call | solution.py:542
  43.5 0.0 collective-permute-done.refs_4_
  43.6 2.6 %shard_map.93 = (f32[8,1,128]{2,1,0:T(1,128)S(1)}, f32[8,64,128]{2,1,0:T(8,128)S(1)}) custom-call(s32[8,32]{1,0:T(8,128)S(1)} %get-tuple-element.29.refs_0_, s32[32]{0:T(128)S(1)} %get-tuple-element.30.refs_1_, s32[8,32]{1,0:T(8,128)S(1)} %get-tuple-element.31.refs_2_, f32[32,8,128]{2,1,0:T(8,128)S(1)} %get-tuple-element.32.refs_3_, ...), custom_call_target="tpu_custom_call" | custom-call | flops 200000000 | bytes 65536 | tf_op jit(solution)/shard_map/pallas_call | solution.py:542
  46.1 0.0 collective-permute-done.1.refs_4_
  46.1 2.6 %shard_map.95 = (f32[8,1,128]{2,1,0:T(1,128)S(1)}, f32[8,64,128]{2,1,0:T(8,128)S(1)}) custom-call(s32[8,32]{1,0:T(8,128)S(1)} %get-tuple-element.29.refs_0_, s32[32]{0:T(128)S(1)} %get-tuple-element.30.refs_1_, s32[8,32]{1,0:T(8,128)S(1)} %get-tuple-element.31.refs_2_, f32[32,8,128]{2,1,0:T(8,128)S(1)} %get-tuple-element.32.refs_3_, ...), custom_call_target="tpu_custom_call" | custom-call | flops 200000000 | bytes 65536 | tf_op jit(solution)/shard_map/pallas_call | solution.py:542
  48.8 0.0 all-to-all-done.1.refs_1_
  48.8 1.6 %shard_map.96 = f32[32,128]{1,0:T(8,128)} custom-call(f32[40,1,128]{2,1,0:T(1,128)S(1)} %all_to_all.10.refs_0_, f32[192,1,128]{2,1,0:T(1,128)S(1)} %all-to-all-done.1.refs_1_, f32[8,64,64]{2,1,0:T(8,128)S(1)} %get-tuple-element.28.refs_2_, f32[8,1,128]{2,1,0:T(1,128)S(1)} %get-tuple-element.35.refs_5_.refs_3_, f32[8,64,128]{2,1,0:T(8,128)S(1)} %get-tuple-element.36.refs_4_, ...), custom_call_target="tpu_custom_call" | custom-call | tf_op jit(solution)/shard_map/pallas_call | solution.py:493
Async XLA Ops:
  17.3 31.5 %all-to-all-start.1 = ((f32[192,1,128]{2,1,0:T(1,128)}), f32[192,1,128]{2,1,0:T(1,128)S(1)}, u32[]{:S(2)}, u32[]{:S(2)}) async-start(f32[192,1,128]{2,1,0:T(1,128)} %get-tuple-element.27), calls=%async_computation.1 | async-start | bytes 196608 | tf_op jit(solution)/shard_map/all_to_all | solution.py:486
  30.0 13.6 %collective-permute-start = (f32[8,8,128]{2,1,0:T(8,128)S(1)}, f32[8,8,128]{2,1,0:T(8,128)S(1)}, u32[]{:S(2)}, u32[]{:S(2)}) collective-permute-start(f32[8,8,128]{2,1,0:T(8,128)S(1)} %get-tuple-element.33.refs_5_), channel_id=1, source_target_pairs={{0,1},{1,2},{2,3},{3,4},{4,5},{5,6},{6,7},{7,8},{8,9},{9,10},{10,1... | collective-permute-start | bytes 98312 | tf_op jit(solution)/shard_map/ppermute | solution.py:480
  32.2 13.9 %collective-permute-start.1 = (f32[8,8,128]{2,1,0:T(8,128)S(1)}, f32[8,8,128]{2,1,0:T(8,128)S(1)}, u32[]{:S(2)}, u32[]{:S(2)}) collective-permute-start(f32[8,8,128]{2,1,0:T(8,128)S(1)} %get-tuple-element.37.refs_4_), channel_id=1, source_target_pairs={{1,0},{2,1},{3,2},{4,3},{5,4},{6,5},{7,6},{8,7},{9,8},{10,9},{11,1... | collective-permute-start | bytes 98312 | tf_op jit(solution)/shard_map/ppermute | solution.py:481

commit v6 on v4

--- a/solution.py
+++ b/solution.py
@@ -147,8 +147,9 @@
             col = jnp.sum(w_ref[i] * other[i : i + 1, :rank] + own, axis=1, keepdims=True)
             total = total + t_ref[i] * col
             pack[i, 4:5, :] = to_row(col, mask2)
-    lo[...] = pack[0:HALO]
-    hi[...] = pack[leaves - HALO : leaves]
+    first = jnp.where(lax.axis_index("gz") % 2 == 0, leaves - HALO, 0)
+    lo[...] = pack[pl.ds(first, HALO)]
+    hi[...] = pack[pl.ds(leaves - HALO - first, HALO)]
     for copy in small[3:]:
         copy.wait()
 
@@ -204,15 +205,13 @@
     token[0] = core
 
 
-def near_kernel(lay, start, near_src, count_src, far_src, pack, halo, after, *refs):
-    del after
-    head = start == 0
+def near_kernel(lay, head, near_src, count_src, far_src, pack, *refs):
     if head:
-        p_ref, t_hbm, w_hbm, near_out, far_out, w_out, node_out, p_s = refs[:8]
-        refs = refs[8:]
+        _, p_ref, t_hbm, w_hbm, near_out, far_out, w_out, node_out, p_s = refs[:9]
+        refs = refs[9:]
     else:
-        t_hbm, near_out, far_out = refs[:3]
-        refs = refs[3:]
+        one, two, _, t_hbm, near_out, far_out = refs[:6]
+        refs = refs[6:]
     near_list, near_count, far_list, win, tgt, acc, t_ref, sem = refs
     leaves, lanes = near_out.shape[0], pack.shape[2]
     rank = lanes // 2
@@ -222,18 +221,25 @@
         (near_src, near_list),
         (count_src, near_count),
         (far_src, far_list),
-        (t_hbm.at[pl.ds(start, leaves)], t_ref),
     ]
+    total = pack.shape[0]
     if head:
+        moves.append((t_hbm.at[pl.ds(HALO, leaves)], t_ref))
         moves.append((w_hbm, w_out))
+    else:
+        moves.append((t_hbm.at[pl.ds(0, HALO)], t_ref.at[pl.ds(0, HALO)]))
+        moves.append((t_hbm.at[pl.ds(total - HALO, HALO)], t_ref.at[pl.ds(HALO, HALO)]))
     copies = [pltpu.make_async_copy(src, dst, sem.at[n]) for n, (src, dst) in enumerate(moves)]
     for copy in copies:
         copy.start()
-    total = pack.shape[0]
-    if head:
-        win[0:HALO] = halo[...]
-    else:
-        win[HALO + total :] = halo[...]
+    if not head:
+        even = lax.axis_index("gz") % 2 == 0
+        win[0:HALO] = jnp.where(even, two[...], one[...])
+        win[HALO + total :] = jnp.where(even, one[...], two[...])
+
+    def name(i):
+        return HALO + i if head else i + (i // HALO) * (total - 2 * HALO)
+
     win[HALO : HALO + total] = pack[...]
 
     pick = lax.broadcasted_iota(jnp.int32, (32, 3 * lanes), 0) % 8
@@ -242,7 +248,7 @@
     used = lax.broadcasted_iota(jnp.int32, (8, lanes), 0) < 3
 
     def spread(i):
-        x = jnp.where(used, win[HALO + start + i], 0.0)
+        x = jnp.where(used, win[HALO + name(i)], 0.0)
         high = x.astype(jnp.bfloat16).astype(jnp.float32)
         rest = x - high
         mid = rest.astype(jnp.bfloat16).astype(jnp.float32)
@@ -288,7 +294,7 @@
             i = g * UNROLL + u
             both = []
             for m in range(0, far_list.shape[0], 2):
-                block = jnp.where(lane < rank, win[far_list[m, start + i]], win[far_list[m + 1, start + i]])
+                block = jnp.where(lane < rank, win[far_list[m, name(i)]], win[far_list[m + 1, name(i)]])
                 both.append([jnp.broadcast_to(block[r : r + 1, :], (8, lanes)) for r in (5, 6, 7, 4)])
             for t in range(far_tiles):
                 far = weighted(i, t, both[0])
@@ -307,15 +313,15 @@
     far_field(groups - 1, False)
 
     def leaf(i, carry):
-        count = near_count[start + i]
+        count = near_count[name(i)]
         for t in range(tiles):
             acc[i, pl.ds(8 * t, 8), :] = jnp.zeros((8, lanes), jnp.float32)
 
         def slots(n, inner):
             m = 2 * n + 1
-            one = rows(near_list[m, start + i], range(4))
+            one = rows(near_list[m, name(i)], range(4))
             then = jnp.minimum(m + 1, near_list.shape[0] - 1)
-            two = rows(near_list[then, start + i], range(4))
+            two = rows(near_list[then, name(i)], range(4))
             two[3] = two[3] * jnp.where(m + 1 < count, 1.0, 0.0)
             for t in range(tiles):
                 at = pl.ds(8 * t, 8)
@@ -325,10 +331,11 @@
         return lax.fori_loop(0, count // 2, slots, carry)
 
     lax.fori_loop(0, leaves, leaf, 0)
-    copies[3].wait()
+    for copy in copies[3:]:
+        copy.wait()
 
     def finish(i, carry):
-        own = rows(near_list[0, start + i], range(4))
+        own = rows(near_list[0, name(i)], range(4))
         sums = [acc[i, pl.ds(8 * t, 8), :] + weighted(i, t, own) for t in range(tiles)]
         whole = jnp.concatenate(sums, axis=0)
         near_out[i] = jnp.sum(jnp.transpose(whole), axis=0, keepdims=True)
@@ -339,11 +346,9 @@
         return carry
 
     lax.fori_loop(0, leaves, finish, 0, unroll=FINISH)
-    for copy in copies[4:]:
-        copy.wait()
-
-
-def post_kernel(lay, recv_a, recv_b, f_ref, near, far, near2, far2, w_ref, node, out, row_s, up_s):
+
+
+def post_kernel(lay, recv_a, recv_b, f_ref, near1, far1, near, far, w_ref, node, out, row_s, up_s):
     leaves, rank = w_ref.shape[0], w_ref.shape[1]
     mask = eye(rank, rank)
     a, b = lay.place()
@@ -392,14 +397,15 @@
     value = value + jnp.sum(carried, axis=1, keepdims=True)
     row = jnp.where(lane < rank, to_row(value, eye(rank, 2 * rank)), 1.0)
 
-    split = far.shape[0]
-    for i in range(leaves):
-        sums = far[i] if i < split else far2[i - split]
-        col = jnp.sum(sums * row, axis=1, keepdims=True)
+    ends, inside = (near1, far1), (near, far)
+    where = [(ends, i) for i in range(HALO)] + [(inside, i) for i in range(leaves - 2 * HALO)]
+    where += [(ends, HALO + i) for i in range(HALO)]
+    for i, (parts, at) in enumerate(where):
+        col = jnp.sum(parts[1][at] * row, axis=1, keepdims=True)
         row_s[i : i + 1, :] = to_row(col, mask)
         up_s[i : i + 1, :] = jnp.sum(w_ref[i] * col, axis=0, keepdims=True)
-    for i in range(leaves):
-        out[i : i + 1, :] = near[i] if i < split else near2[i - split]
+    for i, (parts, at) in enumerate(where):
+        out[i : i + 1, :] = parts[0][at]
     out[...] = out[...] + side(row_s[...], up_s[...])
 
 
@@ -472,27 +478,26 @@
 
     recv_a = lax.all_to_all(send, AXES, 0, 0, axis_index_groups=lay.groups_a(), tiled=True)
     count = lay.na * lay.nb
-    up = [(i, i + 1) for i in range(count - 1)]
-    low = lax.ppermute(hi, AXES, up)
-    high = lax.ppermute(lo, AXES, [(b, a) for a, b in up])
+    one = lax.ppermute(lo, AXES, [(i, i ^ 1) for i in range(count)])
+    links = [(i, i + 1) for i in range(1, count - 1, 2)]
+    two = lax.ppermute(hi, AXES, links + [(j, i) for i, j in links])
 
     send_b, token = call(
         lambda *refs: mid_kernel(lay, *refs), [VM, VM], [vec(lay.nb * lay.rows_b), vec(1)], []
     )(in_vmem(recv_a), in_vmem(msg))
     recv_b = lax.all_to_all(send_b, AXES, 0, 0, axis_index_groups=lay.groups_b(), tiled=True)
 
-    split = leaves - HALO
     near, far, w_ref, node = near_call(
-        lay, 0, split, lists, pack, low, token, p_ref, leaf_transfer, interpolant
+        lay, True, lists, pack, (token, p_ref), leaf_transfer, interpolant
     )
-    near2, far2 = near_call(lay, split, HALO, lists, pack, high, near, p_ref, leaf_transfer, interpolant)
+    near1, far1 = near_call(lay, False, lists, pack, (one, two, near), leaf_transfer, interpolant)
 
     (out,) = call(
         lambda *refs: post_kernel(lay, *refs),
         POST_IN(),
         [jax.ShapeDtypeStruct((leaves, lanes), jnp.float32)],
         POST_SCRATCH(leaves, rank),
-    )(*(in_vmem(x) for x in (recv_a, recv_b, f_ref, near, far, near2, far2, w_ref, node)))
+    )(*(in_vmem(x) for x in (recv_a, recv_b, f_ref, near1, far1, near, far, w_ref, node)))
     return out
 
 
@@ -525,19 +530,19 @@
     )(*(in_hbm(x) for x in (pts, charges, centres, transfers, interpolant, leaf_transfer, *tables)))
 
 
-def near_call(lay, start, leaves, lists, pack, halo, token, p_ref, leaf_transfer, interpolant):
+def near_call(lay, head, lists, pack, others, leaf_transfer, interpolant):
     total, rank = interpolant.shape[0], interpolant.shape[1]
     lanes = pack.shape[2]
-    head = start == 0
+    leaves = total - 2 * HALO if head else 2 * HALO
     outs = [made((leaves, 1, lanes)), made((leaves, rank, lanes))]
     extra = []
     if head:
         outs += [made((total, rank, rank)), made((3 * len(lay.couples), rank, lanes))]
         extra = [pltpu.VMEM((-(-3 * lay.levels // 8) * 8, rank), jnp.float32)]
-    near_inputs = [*lists, pack, halo, token] + ([p_ref] if head else [])
+    near_inputs = [*lists, pack, *others]
     far_inputs = [leaf_transfer] + ([interpolant] if head else [])
     return call(
-        lambda *refs: near_kernel(lay, start, *refs),
+        lambda *refs: near_kernel(lay, head, *refs),
         [VM] * len(near_inputs) + [HB] * len(far_inputs),
         outs,
         [

time: 50.3 us -> 49.3 us (0.980)
  starting transfers between devices: 21.6 us -> 20.8 us
    ppermute x2, starting transfers between devices: 8.88 us -> 8.05 us  [the longest x1 5.8 us: on_device(): two = lax.ppermute(hi, AXES, links + [(j, i) for i, j in links])]
where the time goes in v6:
time: 49.3 us; the launch traced here: 49 us
  starting transfers between devices  20.8 us (42%)
  Pallas kernels  14.1 us (29%)
  blocking collectives  14.1 us (29%)
    all_to_all x1, blocking collectives, on_device(): lax.all_to_all(send, AXES, 0, 0, axis_index_groups=lay.groups_a(), tiled=...  14.1 us
    all_to_all x1, starting transfers between devices, on_device(): lax.all_to_all(send_b, AXES, 0, 0, axis_index_groups=lay.groups_b(), tile...  12.7 us
    pallas_call x2, Pallas kernels, near_call(): call(lambda *refs: near_kernel(lay, head, *refs), [VM] * len(near_inputs)...  9.34 us
    ppermute x1, starting transfers between devices, on_device(): two = lax.ppermute(hi, AXES, links + [(j, i) for i, j in links])  5.8 us
    pallas_call x1, Pallas kernels, call_pre(): call(lambda *refs: pre_kernel(lay, *refs), [HB] * 9, [made((leaves, 8, la...  2.37 us
    ppermute x1, starting transfers between devices, on_device(): one = lax.ppermute(lo, AXES, [(i, i ^ 1) for i in range(count)])  2.25 us
    pallas_call x1, Pallas kernels, on_device(): call(lambda *refs: post_kernel(lay, *refs), POST_IN(), [jax.ShapeDtypeStr...  1.6 us
  transfers between devices with their start and end apart: 3, of which 0 were waited for; matrix products, arithmetic and copies ran while one was open for 0% of the time, Pallas kernels for 19%

profile of v6, /device:TPU:1, one launch (start us, length us, event | category | flops | bytes accessed | tf_op | source)
XLA Modules:
  0.0 49.0 jit_solution(14181582487809279488)
XLA Ops:
  0.0 2.4 %shard_map.91 = (f32[32,8,128]{2,1,0:T(8,128)S(1)}, f32[8,8,128]{2,1,0:T(8,128)S(1)}, f32[8,8,128]{2,1,0:T(8,128)S(1)}, f32[40,1,128]{2,1,0:T(1,128)S(1)}, f32[1...) custom-call(f32[3,32,128]{2,1,0:T(8,128)} %bitcast.6, ...), custom_call_target="tpu_custom_call" | custom-call | tf_op jit(solution)/shard_map/pallas_call | solution.py:509
  2.4 14.1 %all_to_all.10.refs_0_ = f32[40,1,128]{2,1,0:T(1,128)S(1)} all-to-all(f32[40,1,128]{2,1,0:T(1,128)S(1)} %get-tuple-element.23), channel_id=1, replica_groups={{0,1,2,3,32,33,34,35},{4,5,6,7,36,37,38,39},{8,9,10,11,40,41,42,43},{12..., dimensions={0} | all-to-all | bytes 40960 | tf_op jit(solution)/shard_map/all_to_all | solution.py:479
  16.5 0.8 %shard_map.92 = (f32[192,1,128]{2,1,0:T(1,128)}, f32[1,1,128]{2,1,0:T(1,128)S(1)}) custom-call(f32[40,1,128]{2,1,0:T(1,128)S(1)} %all_to_all.10.refs_0_, f32[18,1,128]{2,1,0:T(1,128)S(1)} %get-tuple-element.24.refs_1_), custom_call_target="tpu_custom_call" | custom-call | tf_op jit(solution)/shard_map/pallas_call | solution.py:485
  17.3 12.7 %all-to-all-start.1 = ((f32[192,1,128]{2,1,0:T(1,128)}), f32[192,1,128]{2,1,0:T(1,128)S(1)}, u32[]{:S(2)}, u32[]{:S(2)}) async-start(f32[192,1,128]{2,1,0:T(1,128)} %get-tuple-element.25), calls=%async_computation.1 | async-start | bytes 196608 | tf_op jit(solution)/shard_map/all_to_all | solution.py:488
  30.0 2.2 %collective-permute-start = (f32[8,8,128]{2,1,0:T(8,128)S(1)}, f32[8,8,128]{2,1,0:T(8,128)S(1)}, u32[]{:S(2)}, u32[]{:S(2)}) collective-permute-start(f32[8,8,128]{2,1,0:T(8,128)S(1)} %get-tuple-element.31), channel_id=1, source_target_pairs={{0,1},{1,0},{2,3},{3,2},{4,5},{5,4},{6,7},{7,6},{8,9},{9,8},{10,11... | collective-permute-start | bytes 98312 | tf_op jit(solution)/shard_map/ppermute | solution.py:481
  32.2 5.8 %collective-permute-start.1 = (f32[8,8,128]{2,1,0:T(8,128)S(1)}, f32[8,8,128]{2,1,0:T(8,128)S(1)}, u32[]{:S(2)}, u32[]{:S(2)}) collective-permute-start(f32[8,8,128]{2,1,0:T(8,128)S(1)} %get-tuple-element.32), channel_id=1, source_target_pairs={{1,2},{3,4},{5,6},{7,8},{9,10},{11,12},{13,14},{15,16},{17,18},{19... | collective-permute-start | bytes 98312 | tf_op jit(solution)/shard_map/ppermute | solution.py:483
  38.0 4.7 %shard_map.93 = (f32[16,1,128]{2,1,0:T(1,128)S(1)}, f32[16,64,128]{2,1,0:T(8,128)S(1)}, f32[32,64,64]{2,1,0:T(8,128)S(1)}, f32[15,64,128]{2,1,0:T(8,128)S(1)}) custom-call(s32[8,32]{1,0:T(8,128)S(1)} %get-tuple-element.27.refs_0_, s32[32]{0:T(128)S(1)} %get-tuple-element.28.refs_1_, s32[8,32]{1,0:T(8,128)S(1)} %get-tuple-element.29.refs_2_, ...), custom_call_target="tpu_custom_call" | custom-call | flops 200000000 | bytes 65536 | tf_op jit(solution)/shard_map/pallas_call | solution.py:544
  42.7 0.0 collective-permute-done.refs_4_
  42.7 0.0 collective-permute-done.1.refs_5_
  42.7 4.7 %shard_map.94 = (f32[16,1,128]{2,1,0:T(1,128)S(1)}, f32[16,64,128]{2,1,0:T(8,128)S(1)}) custom-call(s32[8,32]{1,0:T(8,128)S(1)} %get-tuple-element.27.refs_0_, s32[32]{0:T(128)S(1)} %get-tuple-element.28.refs_1_, s32[8,32]{1,0:T(8,128)S(1)} %get-tuple-element.29.refs_2_, f32[32,8,128]{2,1,0:T(8,128)S(1)} %get-tuple-element.30.refs_3_, ...), custom_call_target="tpu_custom_call" | custom-call | flops 200000000 | bytes 65536 | tf_op jit(solution)/shard_map/pallas_call | solution.py:544
  47.4 0.0 all-to-all-done.1.refs_1_
  47.4 1.6 %shard_map.95 = f32[32,128]{1,0:T(8,128)} custom-call(f32[40,1,128]{2,1,0:T(1,128)S(1)} %all_to_all.10.refs_0_, f32[192,1,128]{2,1,0:T(1,128)S(1)} %all-to-all-done.1.refs_1_, f32[8,64,64]{2,1,0:T(8,128)S(1)} %get-tuple-element.26.refs_2_, f32[16,1,128]{2,1,0:T(1,128)S(1)} %get-tuple-element.36.refs_3_, f32[16,64,128]{2,1,0:T(8,128)S(1)} %get-tuple-element.37.refs_4_, ...), custom_call_target="tpu_custom_call" | custom-call | tf_op jit(solution)/shard_map/pallas_call | solution.py:495
Async XLA Ops:
  17.3 30.2 %all-to-all-start.1 = ((f32[192,1,128]{2,1,0:T(1,128)}), f32[192,1,128]{2,1,0:T(1,128)S(1)}, u32[]{:S(2)}, u32[]{:S(2)}) async-start(f32[192,1,128]{2,1,0:T(1,128)} %get-tuple-element.25), calls=%async_computation.1 | async-start | bytes 196608 | tf_op jit(solution)/shard_map/all_to_all | solution.py:488
  30.0 12.8 %collective-permute-start = (f32[8,8,128]{2,1,0:T(8,128)S(1)}, f32[8,8,128]{2,1,0:T(8,128)S(1)}, u32[]{:S(2)}, u32[]{:S(2)}) collective-permute-start(f32[8,8,128]{2,1,0:T(8,128)S(1)} %get-tuple-element.31), channel_id=1, source_target_pairs={{0,1},{1,0},{2,3},{3,2},{4,5},{5,4},{6,7},{7,6},{8,9},{9,8},{10,11... | collective-permute-start | bytes 98312 | tf_op jit(solution)/shard_map/ppermute | solution.py:481
  32.2 10.5 %collective-permute-start.1 = (f32[8,8,128]{2,1,0:T(8,128)S(1)}, f32[8,8,128]{2,1,0:T(8,128)S(1)}, u32[]{:S(2)}, u32[]{:S(2)}) collective-permute-start(f32[8,8,128]{2,1,0:T(8,128)S(1)} %get-tuple-element.32), channel_id=1, source_target_pairs={{1,2},{3,4},{5,6},{7,8},{9,10},{11,12},{13,14},{15,16},{17,18},{19... | collective-permute-start | bytes 98312 | tf_op jit(solution)/shard_map/ppermute | solution.py:483
